TPU v7x, 128 devices: a whole 4x4x4 slice. The times are simulated.
128 devices in a mesh: row: 8 (over y, core), col: 16 (over z, x).
Axes of the slice: x: 4, y: 4, z: 4, core: 2. Of those that a mesh axis runs over, the one named last changes fastest.
Arguments:
- blocks: float32 [32768, 128, 128], P(('row', 'col')), may hold values from -0.25 to 0.25
- block_rows: int32 [128, 256], P(('row', 'col')), may hold values from 0 to 2047, as said below
- block_cols: int32 [128, 256], P(('row', 'col')), may hold values from 0 to 1023
- diagonal: float32 [2097152], P(('row', 'col')), may hold values from 1 to 4
- right_sides: float32 [2, 2097152], P(None, ('row', 'col')), may hold values from -6 to 6
Outputs:
- solution: float32 [2, 2097152], P(None, ('row', 'col'))
- hessenberg: float32 [2, 9, 8], replicated
Inputs may be any that keep to these rules, and one draw needn't show every extreme that they name: `block_rows`: non-decreasing along each tile's slots; a local block row may hold no stored block.
All inputs are finite; a program needn't handle non-finite values.
Results may differ from a plain program's by a relative error of at most 0.0085.
Values sent between devices are 32-bit elements; how exact they have to be, the bound alone decides.
No kernel may reach another device: no remote copies, remote signals or barrier semaphores. Data moves between devices by JAX's collectives and lax.ppermute only.
A program may use at most 128 MiB of HBM per device.

v0:
```python
import functools

import jax
import jax.numpy as jnp
from jax import lax
from jax.sharding import Mesh
from jax.sharding import PartitionSpec as P

STEPS = 8
ROW = ("row_0", "row_1")
COL = ("col_0", "col_1")
ROW_COL = ("row_0", "row_1", "col_0", "col_1")


epsilon = 1e-06


def laid_out(parts, dim):
    dims = list(parts.shape[1:])
    dims[dim] *= parts.shape[0]
    return jnp.moveaxis(parts, 0, dim).reshape(dims)


def from_everyone(value, axis):
    copies = jnp.broadcast_to(value, (lax.axis_size(axis), *value.shape))
    return lax.all_to_all(copies, axis, split_axis=0, concat_axis=0, tiled=True)


def gather_directly(value, axis, dim):
    return laid_out(from_everyone(value, axis), dim)


def in_blocks(value, dim, devices):
    before, after = (value.shape[:dim], value.shape[dim + 1 :])
    return jnp.moveaxis(value.reshape(*before, devices, -1, *after), dim, 0)


def sum_at_owner(value, axis, dim):
    parts = in_blocks(value, dim, lax.axis_size(axis))
    arrived = lax.all_to_all(parts, axis, split_axis=0, concat_axis=0, tiled=True)
    return arrived.sum(axis=0)


def one_axis_at_a_time(value, axes):
    return functools.reduce(lax.psum, axes, value)


def least_squares(hessenberg, initial_norm):
    total_steps = hessenberg.shape[2]
    targets = [initial_norm] + [jnp.zeros_like(initial_norm) for j in range(total_steps)]
    cosines, sines, triangle = ([], [], [])
    for j in range(total_steps):
        column = [hessenberg[:, i, j] for i in range(j + 2)]
        for i in range(j):
            leading, trailing = (column[i], column[i + 1])
            column[i] = cosines[i] * leading + sines[i] * trailing
            column[i + 1] = cosines[i] * trailing - sines[i] * leading
        radius = jnp.sqrt(column[j] * column[j] + column[j + 1] * column[j + 1])
        cosine = column[j] / radius
        sine_term = column[j + 1] / radius
        column[j] = radius
        cosines.append(cosine)
        sines.append(sine_term)
        targets[j + 1] = -sine_term * targets[j]
        targets[j] = cosine * targets[j]
        triangle.append(column[: j + 1])
    coeffs = [None] * total_steps
    for j in reversed(range(total_steps)):
        running = targets[j]
        for k in range(j + 1, total_steps):
            running = running - triangle[k][j] * coeffs[k]
        coeffs[j] = running / triangle[j][j]
    return jnp.stack(coeffs, axis=1)


def apply_matrix(vector, blocks, rows_onehot, block_cols, diagonal):
    systems = vector.shape[0]
    width = blocks.shape[1]
    gathered = gather_directly(vector, ROW, 1)
    grouped = gathered.reshape(systems, -1, width)
    picked = jnp.take(grouped, block_cols, axis=1)
    products = jnp.einsum("kij,nkj->nki", blocks, picked, precision=lax.Precision.HIGHEST)
    own_rows = sum_at_owner(
        jnp.einsum("mk,nki->mni", rows_onehot, products, precision=lax.Precision.HIGHEST), COL, 0
    )
    summed = jnp.transpose(own_rows, (1, 0, 2)).reshape(systems, -1)
    return diagonal[None, :] * vector + summed


def body(blocks, block_rows, block_cols, diagonal, right_sides):
    systems = right_sides.shape[0]
    width = blocks.shape[1]
    row_count = lax.axis_size(COL) * (right_sides.shape[1] // width)
    positions = jnp.arange(row_count, dtype=jnp.int32)
    rows_onehot = (block_rows[0][None, :] == positions[:, None]).astype(jnp.float32)
    columns_local = block_cols[0]
    total_steps = STEPS
    initial_norm = jnp.sqrt(
        one_axis_at_a_time(jnp.sum(right_sides * right_sides, axis=1), ROW_COL) + epsilon
    )
    krylov_basis = [right_sides / initial_norm[:, None]]
    hessenberg = jnp.zeros((systems, total_steps + 1, total_steps), jnp.float32)
    for j in range(total_steps):
        candidate = apply_matrix(krylov_basis[j], blocks, rows_onehot, columns_local, diagonal)
        stacked = jnp.stack(krylov_basis)
        local_dots = jnp.einsum("inl,nl->ni", stacked, candidate, precision=lax.Precision.HIGHEST)
        coeffs, whole_sq = (
            one_axis_at_a_time(local_dots, ROW_COL),
            one_axis_at_a_time(jnp.sum(candidate * candidate, axis=1), ROW_COL),
        )
        candidate = candidate - jnp.einsum(
            "ni,inl->nl", coeffs, stacked, precision=lax.Precision.HIGHEST
        )
        remainder_sq = jnp.maximum(whole_sq - jnp.sum(coeffs * coeffs, axis=1), 0.01 * whole_sq)
        new_norm = jnp.sqrt(remainder_sq + epsilon)
        hessenberg = hessenberg.at[:, : j + 1, j].set(coeffs)
        hessenberg = hessenberg.at[:, j + 1, j].set(new_norm)
        krylov_basis.append(candidate / new_norm[:, None])
    weights = least_squares(hessenberg, initial_norm)
    solution = jnp.einsum(
        "ni,inl->nl",
        weights,
        jnp.stack(krylov_basis[:total_steps]),
        precision=lax.Precision.HIGHEST,
    )
    return (solution, hessenberg)


def solution(mesh):
    finer = Mesh(mesh.devices.reshape(4, 2, 4, 4), ("row_0", "row_1", "col_0", "col_1"))
    placed = (
        P(ROW_COL, None, None),
        P(ROW_COL, None),
        P(ROW_COL, None),
        P(ROW_COL),
        P(None, ROW_COL),
    )
    return jax.shard_map(
        body, mesh=finer, in_specs=placed, out_specs=(P(None, ROW_COL), P()), check_vma=False
    )
```

profile of v0, /device:TPU:1, one launch (start us, length us, event | category | flops | bytes accessed | tf_op | source)
XLA Modules:
  0.0 1011.4 jit_solution(11837457509341287643)
XLA Ops:
  16.1 9.7 psum.478
  45.2 15.0 %all-to-all-done = f32[8,2,16384]{2,1,0:T(2,128)S(1)} async-done(((f32[8,2,16384]{2,1,0:T(2,128)}), f32[8,2,16384]{2,1,0:T(2,128)S(1)}, u32[]{:S(2)}, u32[]{:S(2)}) %all-to-all-start) | async-done | bytes 1048608 | tf_op jit(solution)/shard_map/all_to_all | solution.py:26
  61.1 28.7 %convolution_bitcast_fusion.7 = f32[2,256,128]{2,0,1:T(2,128)S(1)} fusion(f32[256,128,128]{2,1,0:T(8,128)} %param.39, f32[256,2,128]{2,1,0:T(2,128)S(1)} %gather_fusion, pred[256]{0:T(512)(128)(4,1)S(1)} %compare_and_fusion), kind=kOutput, calls=%fused_computation.29 | convolution fusion | flops 100728832 | bytes 17301760 | tf_op jit(solution)/shard_map/kij,nkj->nki/dot_general | solution.py:82
  91.2 29.9 %all_to_all.80 = f32[16,128,2,128]{3,1,2,0:T(8,128)S(1)} all-to-all(f32[16,128,2,128]{3,1,2,0:T(8,128)S(1)} %copy.34), channel_id=1, replica_groups=mesh['row_0'=4,'row_1'=2,'col_0'=4,'col_1'=4] {'col_0','col_1'}, dimensions={0} | all-to-all | bytes 4194304 | tf_op jit(solution)/shard_map/all_to_all | solution.py:40
  149.6 22.2 %all_to_all.81 = f32[8,2,16384]{2,1,0:T(2,128)S(1)} all-to-all(f32[8,2,16384]{2,1,0:T(2,128)S(1)} %broadcast_in_dim.26), channel_id=1, replica_groups=mesh['row_0'=4,'row_1'=2,'col_0'=4,'col_1'=4] {'row_0','row_1'}, dimensions={0} | all-to-all | bytes 2097152 | tf_op jit(solution)/shard_map/all_to_all | solution.py:26
  172.8 28.7 %convolution_bitcast_fusion.6 = f32[2,256,128]{2,0,1:T(2,128)S(1)} fusion(f32[256,128,128]{2,1,0:T(8,128)} %param.39, f32[256,2,128]{2,1,0:T(2,128)S(1)} %gather_fusion.1, pred[256]{0:T(512)(128)(4,1)S(1)} %compare_and_fusion), kind=kOutput, calls=%fused_computation.28 | convolution fusion | flops 100728832 | bytes 17301760 | tf_op jit(solution)/shard_map/kij,nkj->nki/dot_general | solution.py:82
  208.0 30.3 %all-to-all-done.3 = f32[16,128,2,128]{3,1,2,0:T(8,128)S(1)} async-done(((f32[16,128,2,128]{3,1,2,0:T(8,128)}), f32[16,128,2,128]{3,1,2,0:T(8,128)S(1)}, u32[]{:S(2)}, u32[]{:S(2)}) %all-to-all-start.3) | async-done | bytes 2097184 | tf_op jit(solution)/shard_map/all_to_all | solution.py:40
  269.8 21.6 %all_to_all.82 = f32[8,2,16384]{2,1,0:T(2,128)S(1)} all-to-all(f32[8,2,16384]{2,1,0:T(2,128)S(1)} %broadcast_in_dim.27), channel_id=1, replica_groups=mesh['row_0'=4,'row_1'=2,'col_0'=4,'col_1'=4] {'row_0','row_1'}, dimensions={0} | all-to-all | bytes 2097152 | tf_op jit(solution)/shard_map/all_to_all | solution.py:26
  292.5 28.7 %convolution_bitcast_fusion.5 = f32[2,256,128]{2,0,1:T(2,128)S(1)} fusion(f32[256,128,128]{2,1,0:T(8,128)} %param.39, f32[256,2,128]{2,1,0:T(2,128)S(1)} %gather_fusion.2, pred[256]{0:T(512)(128)(4,1)S(1)} %compare_and_fusion), kind=kOutput, calls=%fused_computation.27 | convolution fusion | flops 100728832 | bytes 17301760 | tf_op jit(solution)/shard_map/kij,nkj->nki/dot_general | solution.py:82
  328.5 29.4 %all-to-all-done.5 = f32[16,128,2,128]{3,1,2,0:T(8,128)S(1)} async-done(((f32[16,128,2,128]{3,1,2,0:T(8,128)}), f32[16,128,2,128]{3,1,2,0:T(8,128)S(1)}, u32[]{:S(2)}, u32[]{:S(2)}) %all-to-all-start.5) | async-done | bytes 2097184 | tf_op jit(solution)/shard_map/all_to_all | solution.py:40
  401.1 14.1 %all-to-all-done.6 = f32[8,2,16384]{2,1,0:T(2,128)S(1)} async-done(((f32[8,2,16384]{2,1,0:T(2,128)}), f32[8,2,16384]{2,1,0:T(2,128)S(1)}, u32[]{:S(2)}, u32[]{:S(2)}) %all-to-all-start.6) | async-done | bytes 1048608 | tf_op jit(solution)/shard_map/all_to_all | solution.py:26
  416.2 28.7 %convolution_bitcast_fusion.4 = f32[2,256,128]{2,0,1:T(2,128)S(1)} fusion(f32[256,128,128]{2,1,0:T(8,128)} %param.39, f32[256,2,128]{2,1,0:T(2,128)S(1)} %gather_fusion.3, pred[256]{0:T(512)(128)(4,1)S(1)} %compare_and_fusion), kind=kOutput, calls=%fused_computation.26 | convolution fusion | flops 100728832 | bytes 17301760 | tf_op jit(solution)/shard_map/kij,nkj->nki/dot_general | solution.py:82
  453.1 29.1 %all-to-all-done.7 = f32[16,128,2,128]{3,1,2,0:T(8,128)S(1)} async-done(((f32[16,128,2,128]{3,1,2,0:T(8,128)}), f32[16,128,2,128]{3,1,2,0:T(8,128)S(1)}, u32[]{:S(2)}, u32[]{:S(2)}) %all-to-all-start.7) | async-done | bytes 2097184 | tf_op jit(solution)/shard_map/all_to_all | solution.py:40
  525.6 14.2 %all-to-all-done.8 = f32[8,2,16384]{2,1,0:T(2,128)S(1)} async-done(((f32[8,2,16384]{2,1,0:T(2,128)}), f32[8,2,16384]{2,1,0:T(2,128)S(1)}, u32[]{:S(2)}, u32[]{:S(2)}) %all-to-all-start.8) | async-done | bytes 1048608 | tf_op jit(solution)/shard_map/all_to_all | solution.py:26
  540.8 28.7 %convolution_bitcast_fusion.3 = f32[2,256,128]{2,0,1:T(2,128)S(1)} fusion(f32[256,128,128]{2,1,0:T(8,128)} %param.39, f32[256,2,128]{2,1,0:T(2,128)S(1)} %gather_fusion.4, pred[256]{0:T(512)(128)(4,1)S(1)} %compare_and_fusion), kind=kOutput, calls=%fused_computation.25 | convolution fusion | flops 100728832 | bytes 17301760 | tf_op jit(solution)/shard_map/kij,nkj->nki/dot_general | solution.py:82
  577.4 29.3 %all-to-all-done.9 = f32[16,128,2,128]{3,1,2,0:T(8,128)S(1)} async-done(((f32[16,128,2,128]{3,1,2,0:T(8,128)}), f32[16,128,2,128]{3,1,2,0:T(8,128)S(1)}, u32[]{:S(2)}, u32[]{:S(2)}) %all-to-all-start.9) | async-done | bytes 2097184 | tf_op jit(solution)/shard_map/all_to_all | solution.py:40
  640.0 21.6 %all_to_all.83 = f32[8,2,16384]{2,1,0:T(2,128)S(1)} all-to-all(f32[8,2,16384]{2,1,0:T(2,128)S(1)} %broadcast_in_dim.30), channel_id=1, replica_groups=mesh['row_0'=4,'row_1'=2,'col_0'=4,'col_1'=4] {'row_0','row_1'}, dimensions={0} | all-to-all | bytes 2097152 | tf_op jit(solution)/shard_map/all_to_all | solution.py:26
  662.6 28.7 %convolution_bitcast_fusion.2 = f32[2,256,128]{2,0,1:T(2,128)S(1)} fusion(f32[256,128,128]{2,1,0:T(8,128)} %param.39, f32[256,2,128]{2,1,0:T(2,128)S(1)} %gather_fusion.5, pred[256]{0:T(512)(128)(4,1)S(1)} %compare_and_fusion), kind=kOutput, calls=%fused_computation.24 | convolution fusion | flops 100728832 | bytes 17301760 | tf_op jit(solution)/shard_map/kij,nkj->nki/dot_general | solution.py:82
  698.4 29.7 %all-to-all-done.11 = f32[16,128,2,128]{3,1,2,0:T(8,128)S(1)} async-done(((f32[16,128,2,128]{3,1,2,0:T(8,128)}), f32[16,128,2,128]{3,1,2,0:T(8,128)S(1)}, u32[]{:S(2)}, u32[]{:S(2)}) %all-to-all-start.11) | async-done | bytes 2097184 | tf_op jit(solution)/shard_map/all_to_all | solution.py:40
  760.3 21.9 %all_to_all.84 = f32[8,2,16384]{2,1,0:T(2,128)S(1)} all-to-all(f32[8,2,16384]{2,1,0:T(2,128)S(1)} %broadcast_in_dim.31), channel_id=1, replica_groups=mesh['row_0'=4,'row_1'=2,'col_0'=4,'col_1'=4] {'row_0','row_1'}, dimensions={0} | all-to-all | bytes 2097152 | tf_op jit(solution)/shard_map/all_to_all | solution.py:26
  783.1 28.7 %convolution_bitcast_fusion.1 = f32[2,256,128]{2,0,1:T(2,128)S(1)} fusion(f32[256,128,128]{2,1,0:T(8,128)} %param.39, f32[256,2,128]{2,1,0:T(2,128)S(1)} %gather_fusion.6, pred[256]{0:T(512)(128)(4,1)S(1)} %compare_and_fusion), kind=kOutput, calls=%fused_computation.23 | convolution fusion | flops 100728832 | bytes 17301760 | tf_op jit(solution)/shard_map/kij,nkj->nki/dot_general | solution.py:82
  818.4 30.3 %all-to-all-done.13 = f32[16,128,2,128]{3,1,2,0:T(8,128)S(1)} async-done(((f32[16,128,2,128]{3,1,2,0:T(8,128)}), f32[16,128,2,128]{3,1,2,0:T(8,128)S(1)}, u32[]{:S(2)}, u32[]{:S(2)}) %all-to-all-start.13) | async-done | bytes 2097184 | tf_op jit(solution)/shard_map/all_to_all | solution.py:40
  891.8 13.1 %all-to-all-done.14 = f32[8,2,16384]{2,1,0:T(2,128)S(1)} async-done(((f32[8,2,16384]{2,1,0:T(2,128)}), f32[8,2,16384]{2,1,0:T(2,128)S(1)}, u32[]{:S(2)}, u32[]{:S(2)}) %all-to-all-start.14) | async-done | bytes 1048608 | tf_op jit(solution)/shard_map/all_to_all | solution.py:26
  905.8 28.7 %convolution_bitcast_fusion = f32[2,256,128]{2,0,1:T(2,128)S(1)} fusion(f32[256,128,128]{2,1,0:T(8,128)} %param.39, f32[256,2,128]{2,1,0:T(2,128)S(1)} %gather_fusion.7, pred[256]{0:T(512)(128)(4,1)S(1)} %compare_and_fusion), kind=kOutput, calls=%fused_computation.22 | convolution fusion | flops 100728832 | bytes 17301760 | tf_op jit(solution)/shard_map/kij,nkj->nki/dot_general | solution.py:82
  (283 shorter events, 418.5 us)
Async XLA Ops:
  0.6 44.5 %copy-start.29 = (s32[1,256]{1,0:T(1,128)S(1)}, s32[1,256]{1,0:T(1,128)}, u32[]{:S(2)}) copy-start(s32[1,256]{1,0:T(1,128)} %param.41) | copy-start | bytes 3076
  37.3 22.8 %all-to-all-start = ((f32[8,2,16384]{2,1,0:T(2,128)}), f32[8,2,16384]{2,1,0:T(2,128)S(1)}, u32[]{:S(2)}, u32[]{:S(2)}) async-start(f32[8,2,16384]{2,1,0:T(2,128)} %broadcast_in_dim.25), calls=%async_computation | async-start | bytes 2097152 | tf_op jit(solution)/shard_map/all_to_all | solution.py:26
  61.1 28.8 %copy-start.8 = (s32[1,256]{1,0:T(1,128)S(1)}, s32[1,256]{1,0:T(1,128)}, u32[]{:S(2)}) copy-start(s32[1,256]{1,0:T(1,128)} %param.40) | copy-start | bytes 3076
  148.4 23.4 %copy-start.15 = (f32[2,1]{0,1:T(1,128)}, f32[2,1]{0,1:T(1,128)S(1)}, u32[]{:S(2)}) copy-start(f32[2,1]{0,1:T(1,128)S(1)} %get-tuple-element.217) | copy-start | bytes 28
  148.4 23.4 %copy-start.19 = (f32[2]{0:T(128)}, f32[2]{0:T(128)S(1)}, u32[]{:S(2)}) copy-start(f32[2]{0:T(128)S(1)} %fusion.108) | copy-start | bytes 28
  204.1 34.1 %all-to-all-start.3 = ((f32[16,128,2,128]{3,1,2,0:T(8,128)}), f32[16,128,2,128]{3,1,2,0:T(8,128)S(1)}, u32[]{:S(2)}, u32[]{:S(2)}) async-start(f32[16,128,2,128]{3,1,2,0:T(8,128)} %copy.38), calls=%async_computation.3 | async-start | bytes 4194304 | tf_op jit(solution)/shard_map/all_to_all | solution.py:40
  267.5 23.9 %copy-start.30 = (f32[2,2]{1,0:T(2,128)}, f32[2,2]{1,0:T(2,128)S(1)}, u32[]{:S(2)}) copy-start(f32[2,2]{1,0:T(2,128)S(1)} %get-tuple-element.215) | copy-start | bytes 52
  268.8 23.7 %copy-start.21 = (f32[2]{0:T(128)}, f32[2]{0:T(128)S(1)}, u32[]{:S(2)}) copy-start(f32[2]{0:T(128)S(1)} %add_sqrt_fusion.13) | copy-start | bytes 28
  323.8 34.1 %all-to-all-start.5 = ((f32[16,128,2,128]{3,1,2,0:T(8,128)}), f32[16,128,2,128]{3,1,2,0:T(8,128)S(1)}, u32[]{:S(2)}, u32[]{:S(2)}) async-start(f32[16,128,2,128]{3,1,2,0:T(8,128)} %copy.43), calls=%async_computation.5 | async-start | bytes 4194304 | tf_op jit(solution)/shard_map/all_to_all | solution.py:40
  391.2 91.1 %copy-start.5 = (f32[2,16384]{1,0:T(2,128)}, f32[2,16384]{1,0:T(2,128)S(1)}, u32[]{:S(2)}) copy-start(f32[2,16384]{1,0:T(2,128)S(1)} %get-tuple-element.325) | copy-start | bytes 393220
  392.5 22.8 %all-to-all-start.6 = ((f32[8,2,16384]{2,1,0:T(2,128)}), f32[8,2,16384]{2,1,0:T(2,128)S(1)}, u32[]{:S(2)}, u32[]{:S(2)}) async-start(f32[8,2,16384]{2,1,0:T(2,128)} %broadcast_in_dim.28), calls=%async_computation.6 | async-start | bytes 2097152 | tf_op jit(solution)/shard_map/all_to_all | solution.py:26
  447.6 34.6 %all-to-all-start.7 = ((f32[16,128,2,128]{3,1,2,0:T(8,128)}), f32[16,128,2,128]{3,1,2,0:T(8,128)S(1)}, u32[]{:S(2)}, u32[]{:S(2)}) async-start(f32[16,128,2,128]{3,1,2,0:T(8,128)} %copy.48), calls=%async_computation.7 | async-start | bytes 4194304 | tf_op jit(solution)/shard_map/all_to_all | solution.py:40
  515.5 25.2 %copy-start.7 = (f32[2,16384]{1,0:T(2,128)}, f32[2,16384]{1,0:T(2,128)S(1)}, u32[]{:S(2)}) copy-start(f32[2,16384]{1,0:T(2,128)S(1)} %get-tuple-element.323) | copy-start | bytes 393220
  516.8 23.0 %all-to-all-start.8 = ((f32[8,2,16384]{2,1,0:T(2,128)}), f32[8,2,16384]{2,1,0:T(2,128)S(1)}, u32[]{:S(2)}, u32[]{:S(2)}) async-start(f32[8,2,16384]{2,1,0:T(2,128)} %broadcast_in_dim.29), calls=%async_computation.8 | async-start | bytes 2097152 | tf_op jit(solution)/shard_map/all_to_all | solution.py:26
  572.1 34.6 %all-to-all-start.9 = ((f32[16,128,2,128]{3,1,2,0:T(8,128)}), f32[16,128,2,128]{3,1,2,0:T(8,128)S(1)}, u32[]{:S(2)}, u32[]{:S(2)}) async-start(f32[16,128,2,128]{3,1,2,0:T(8,128)} %copy.53), calls=%async_computation.9 | async-start | bytes 4194304 | tf_op jit(solution)/shard_map/all_to_all | solution.py:40
  638.9 22.7 %copy-start.27 = (f32[2]{0:T(128)}, f32[2]{0:T(128)S(1)}, u32[]{:S(2)}) copy-start(f32[2]{0:T(128)S(1)} %add_sqrt_fusion.10) | copy-start | bytes 28
  693.9 34.1 %all-to-all-start.11 = ((f32[16,128,2,128]{3,1,2,0:T(8,128)}), f32[16,128,2,128]{3,1,2,0:T(8,128)S(1)}, u32[]{:S(2)}, u32[]{:S(2)}) async-start(f32[16,128,2,128]{3,1,2,0:T(8,128)} %copy.58), calls=%async_computation.11 | async-start | bytes 4194304 | tf_op jit(solution)/shard_map/all_to_all | solution.py:40
  697.6 30.5 %copy-start.3 = (f32[16384]{0:T(1024)S(1)}, f32[16384]{0:T(1024)}, u32[]{:S(2)}) copy-start(f32[16384]{0:T(1024)} %param.42) | copy-start | bytes 196612
  757.7 24.5 %copy-start.13 = (f32[2,6]{1,0:T(2,128)}, f32[2,6]{1,0:T(2,128)S(1)}, u32[]{:S(2)}) copy-start(f32[2,6]{1,0:T(2,128)S(1)} %get-tuple-element.207) | copy-start | bytes 148
  814.5 34.2 %all-to-all-start.13 = ((f32[16,128,2,128]{3,1,2,0:T(8,128)}), f32[16,128,2,128]{3,1,2,0:T(8,128)S(1)}, u32[]{:S(2)}, u32[]{:S(2)}) async-start(f32[16,128,2,128]{3,1,2,0:T(8,128)} %copy.63), calls=%async_computation.13 | async-start | bytes 4194304 | tf_op jit(solution)/shard_map/all_to_all | solution.py:40
  818.3 30.5 %copy-start.4 = (f32[16384]{0:T(1024)S(1)}, f32[16384]{0:T(1024)}, u32[]{:S(2)}) copy-start(f32[16384]{0:T(1024)} %param.42) | copy-start | bytes 196612
  882.1 22.7 %all-to-all-start.14 = ((f32[8,2,16384]{2,1,0:T(2,128)}), f32[8,2,16384]{2,1,0:T(2,128)S(1)}, u32[]{:S(2)}, u32[]{:S(2)}) async-start(f32[8,2,16384]{2,1,0:T(2,128)} %broadcast_in_dim.58), calls=%async_computation.14 | async-start | bytes 2097152 | tf_op jit(solution)/shard_map/all_to_all | solution.py:26
  937.3 34.8 %all-to-all-start.15 = ((f32[16,128,2,128]{3,1,2,0:T(8,128)}), f32[16,128,2,128]{3,1,2,0:T(8,128)S(1)}, u32[]{:S(2)}, u32[]{:S(2)}) async-start(f32[16,128,2,128]{3,1,2,0:T(8,128)} %copy.68), calls=%async_computation.15 | async-start | bytes 4194304 | tf_op jit(solution)/shard_map/all_to_all | solution.py:40
  947.6 59.2 %copy-start.18 = (f32[2]{0:T(128)S(1)}, f32[2]{0:T(128)}, u32[]{:S(2)}) copy-start(f32[2]{0:T(128)} %copy-done.17) | copy-start | bytes 28
  (25 other events, 228.7 us)
where the time goes:
time: 1020 us; the launch traced here: 1010 us
  blocking collectives  360 us (35%)
  matrix products  273 us (27%)
  waiting for transfers between devices  242 us (24%)
  starting transfers between devices  57.7 us (6%)
  local copies, waits for them, and re-layouts  46.8 us (5%)
  other arithmetic  30.2 us (3%)
    psum x36, blocking collectives, one_axis_at_a_time(): return functools.reduce(lax.psum, axes, value)  242 us
    dot_general x8, matrix products, apply_matrix(): jnp.einsum('kij,nkj->nki', blocks, picked, precision=lax.Precision.HIGHEST)  230 us
    all_to_all x7, waiting for transfers between devices, sum_at_owner(): lax.all_to_all(parts, axis, split_axis=0, concat_axis=0, tiled=True)  186 us
    all_to_all x4, blocking collectives, from_everyone(): return lax.all_to_all(copies, axis, split_axis=0, concat_axis=0, tiled=True)  87.3 us
    all_to_all x4, waiting for transfers between devices, from_everyone(): return lax.all_to_all(copies, axis, split_axis=0, concat_axis=0, tiled=True)  56.3 us
    all_to_all x4, starting transfers between devices, from_everyone(): return lax.all_to_all(copies, axis, split_axis=0, concat_axis=0, tiled=True)  31.4 us
    all_to_all x1, blocking collectives, sum_at_owner(): lax.all_to_all(parts, axis, split_axis=0, concat_axis=0, tiled=True)  29.9 us
    all_to_all x7, starting transfers between devices, sum_at_owner(): lax.all_to_all(parts, axis, split_axis=0, concat_axis=0, tiled=True)  26.3 us
  transfers between devices with their start and end apart: 11, of which 11 were waited for; matrix products, arithmetic and copies ran while one was open for 3% of the time, Pallas kernels for 0%

commit v1 on v0

v1 whole, which is shorter than its diff:
```python
import functools

import jax
import jax.numpy as jnp
from jax import lax
from jax.experimental import pallas as pl
from jax.experimental.pallas import tpu as pltpu
from jax.sharding import PartitionSpec as P

STEPS = 8
BS = 128
SRC_SLOTS = 56
DST_SLOTS = 24
ROW = "row"
COL = "col"
BOTH = ("row", "col")
F32 = jnp.float32
BF16 = jnp.bfloat16

epsilon = 1e-06

QQ, PP, GRAM, FLAG = 9, 10, 16, 127


def swap(value, axis):
    return lax.all_to_all(value, axis, split_axis=0, concat_axis=0, tiled=True)


def least_squares(hessenberg, initial_norm):
    total_steps = hessenberg.shape[2]
    targets = [initial_norm] + [jnp.zeros_like(initial_norm) for j in range(total_steps)]
    cosines, sines, triangle = ([], [], [])
    for j in range(total_steps):
        column = [hessenberg[:, i, j] for i in range(j + 2)]
        rotate(column, cosines, sines, targets, triangle)
    return jnp.stack(back_substitute(triangle, targets), axis=1)


def rotate(column, cosines, sines, targets, triangle):
    j = len(column) - 2
    for i in range(j):
        leading, trailing = (column[i], column[i + 1])
        column[i] = cosines[i] * leading + sines[i] * trailing
        column[i + 1] = cosines[i] * trailing - sines[i] * leading
    radius = jnp.sqrt(column[j] * column[j] + column[j + 1] * column[j + 1])
    cosine = column[j] / radius
    sine_term = column[j + 1] / radius
    column[j] = radius
    cosines.append(cosine)
    sines.append(sine_term)
    targets[j + 1] = -sine_term * targets[j]
    targets[j] = cosine * targets[j]
    triangle.append(column[: j + 1])


def back_substitute(triangle, targets):
    total_steps = len(triangle)
    coeffs = [None] * total_steps
    for j in reversed(range(total_steps)):
        running = targets[j]
        for k in range(j + 1, total_steps):
            running = running - triangle[k][j] * coeffs[k]
        coeffs[j] = running / triangle[j][j]
    return coeffs


def dense_cycle(blocks, block_rows, block_cols, diagonal, right_sides):
    systems = right_sides.shape[0]
    groups = lax.axis_size(COL)
    length = right_sides.shape[1]
    row_count = groups * (length // BS)
    positions = jnp.arange(row_count, dtype=jnp.int32)
    onehot = (block_rows[0][None, :] == positions[:, None]).astype(F32)
    high = lax.Precision.HIGHEST

    def everywhere(value):
        return lax.psum(lax.psum(value, ROW), COL)

    def apply_matrix(vector):
        copies = jnp.broadcast_to(vector, (lax.axis_size(ROW), *vector.shape))
        gathered = jnp.moveaxis(swap(copies, ROW), 0, 1).reshape(systems, -1, BS)
        picked = jnp.take(gathered, block_cols[0], axis=1)
        products = jnp.einsum("kij,nkj->nki", blocks, picked, precision=high)
        partial = jnp.einsum("mk,nki->mni", onehot, products, precision=high)
        own = swap(partial.reshape(groups, -1, systems, BS), COL).sum(axis=0)
        return diagonal[None, :] * vector + jnp.transpose(own, (1, 0, 2)).reshape(systems, -1)

    def norm(vector):
        return jnp.sqrt(everywhere(jnp.sum(vector * vector, axis=1)) + epsilon)

    initial_norm = norm(right_sides)
    basis = jnp.zeros((STEPS + 1, systems, length), F32).at[0].set(right_sides / initial_norm[:, None])
    hessenberg = jnp.zeros((systems, STEPS + 1, STEPS), F32)

    def step(j, state):
        basis, hessenberg = state
        candidate = apply_matrix(basis[j])
        coeffs = everywhere(jnp.einsum("inl,nl->ni", basis, candidate, precision=high))
        candidate = candidate - jnp.einsum("ni,inl->nl", coeffs, basis, precision=high)
        new_norm = norm(candidate)
        below = (jnp.arange(STEPS + 1) == j + 1).astype(F32)
        column = coeffs + below[None, :] * new_norm[:, None]
        here = (jnp.arange(STEPS) == j).astype(F32)
        hessenberg = hessenberg + column[:, :, None] * here[None, None, :]
        basis = basis.at[j + 1].set(candidate / new_norm[:, None])
        return basis, hessenberg

    basis, hessenberg = lax.fori_loop(0, STEPS, step, (basis, hessenberg))
    weights = least_squares(hessenberg, initial_norm)
    solution = jnp.einsum("ni,inl->nl", weights, basis[:STEPS], precision=high)
    return solution, hessenberg


def whole(count):
    return [pl.BlockSpec(memory_space=pltpu.VMEM)] * count


def call(kernel, outs, operands, scratch=(), vmem=24 << 20, name=None):
    return pl.pallas_call(
        kernel,
        out_shape=outs,
        in_specs=whole(len(operands)),
        out_specs=jax.tree.map(lambda o: pl.BlockSpec(memory_space=pltpu.VMEM), outs),
        scratch_shapes=list(scratch),
        compiler_params=pltpu.CompilerParams(vmem_limit_bytes=vmem),
        name=name,
    )(*operands)


def pieces(value, count):
    out = []
    for _ in range(count):
        piece = value.astype(BF16)
        out.append(piece)
        value = value - piece.astype(F32)
    return out


def pick(selector, value, count=3):
    return sum(jnp.dot(selector, piece, preferred_element_type=F32) for piece in pieces(value, count))


def turn_kernel(blocks_ref, turned_ref):
    for pair in range(turned_ref.shape[0]):
        for half in range(2):
            turned_ref[pair, :, half * BS : (half + 1) * BS] = blocks_ref[2 * pair + half].T.astype(BF16)


def turn_blocks(blocks, per_step=16):
    count = blocks.shape[0]
    return pl.pallas_call(
        turn_kernel,
        out_shape=jax.ShapeDtypeStruct((count // 2, BS, 2 * BS), BF16),
        grid=(count // per_step,),
        in_specs=[pl.BlockSpec((per_step, BS, BS), lambda i: (i, 0, 0))],
        out_specs=pl.BlockSpec((per_step // 2, BS, 2 * BS), lambda i: (i, 0, 0)),
        compiler_params=pltpu.CompilerParams(vmem_limit_bytes=8 << 20),
        name="turn_blocks",
    )(blocks)


def product_kernel(extra, *refs):
    if extra:
        got_ref, spread_ref, turned_ref, sums_ref, extra_ref, out_ref, left_ref, prod_ref = refs
    else:
        got_ref, spread_ref, turned_ref, sums_ref, out_ref, left_ref, prod_ref = refs
    sources, slots = got_ref.shape[0], got_ref.shape[1]
    targets, target_slots = out_ref.shape[0], out_ref.shape[1]
    got = got_ref[...].reshape(sources * slots, 2 * BS)
    count = spread_ref.shape[0]
    for at, piece in enumerate(pieces(got, 2)):
        picked = jnp.dot(spread_ref[...], piece, preferred_element_type=F32)
        left_ref[pl.ds(2 * at, count, stride=4), :] = picked[:, :BS]
        left_ref[pl.ds(2 * at + 1, count, stride=4), :] = picked[:, BS:]
    first = lax.broadcasted_iota(jnp.int32, (8, BS), 0) < 4

    def pair_step(pair, carry):
        rows = pl.ds(pl.multiple_of(8 * pair, 8), 8)
        both = jnp.dot(left_ref[rows, :].astype(BF16), turned_ref[pair], preferred_element_type=F32)
        prod_ref[rows, :] = jnp.where(first, both[:, :BS], both[:, BS:])
        return carry

    lax.fori_loop(0, turned_ref.shape[0], pair_step, 0, unroll=16)
    products = jnp.concatenate(
        [prod_ref[pl.ds(n, count, stride=4), :] + prod_ref[pl.ds(n + 2, count, stride=4), :] for n in range(2)],
        axis=1,
    )
    summed = pick(sums_ref[...], products)
    out_ref[...] = summed.reshape(targets, target_slots, 2 * BS)
    ride = got_ref[0, slots - 1 : slots, :]
    for s in range(1, sources):
        ride = ride + got_ref[s, slots - 1 : slots, :]
    for t in range(targets):
        row = ride + extra_ref[t : t + 1, :] if extra else ride
        out_ref[t, target_slots - 1 : target_slots, :] = row


def block_products(got, spread, turned, sums, extra=None):
    operands = (got, spread, turned, sums) + ((extra,) if extra is not None else ())
    count = spread.shape[0]
    targets = sums.shape[0] // DST_SLOTS
    return call(
        functools.partial(product_kernel, extra is not None),
        jax.ShapeDtypeStruct((targets, DST_SLOTS, 2 * BS), F32),
        operands,
        [pltpu.VMEM((4 * count, BS), F32), pltpu.VMEM((4 * count, BS), F32)],
        vmem=16 << 20,
        name="block_products",
    )


def lane_of(row, lane):
    return row[:, lane : lane + 1]


def total(value):
    return jnp.sum(value, axis=0, keepdims=True)


def send_out(values, wanted_ref, ride, out_ref):
    out = pick(wanted_ref[...], values)
    out_ref[...] = out.reshape(out_ref.shape)
    slots = out_ref.shape[1]
    for s in range(out_ref.shape[0]):
        out_ref[s, slots - 1 : slots, :] = ride


def start_kernel(b_ref, wanted_ref, ride_ref, out_ref):
    values = jnp.concatenate([b_ref[0], b_ref[1]], axis=1)
    send_out(values, wanted_ref, ride_ref[0:1, :], out_ref)


def inner_products(dots_ref, vs, q, p, j):
    rides = []
    for n in range(2):
        cut = slice(n * BS, (n + 1) * BS)
        dots_ref[...] = jnp.zeros(dots_ref.shape, F32)
        qn, pn = q[:, cut], p[:, cut]
        for i in range(j):
            vn = vs[i][:, cut]
            dots_ref[i : i + 1, :] = total(vn * pn)
            dots_ref[GRAM + i : GRAM + i + 1, :] = total(vn * qn)
        dots_ref[j : j + 1, :] = total(qn * pn)
        dots_ref[QQ : QQ + 1, :] = total(qn * qn)
        dots_ref[PP : PP + 1, :] = total(pn * pn)
        ones = jnp.ones((8, BS), F32)
        row = lax.dot_general(
            ones, dots_ref[...], (((1,), (1,)), ((), ())),
            precision=lax.Precision.HIGHEST, preferred_element_type=F32,
        )
        rides.append(row[0:1, :])
    return jnp.concatenate(rides, axis=1)


def arrived(got_ref, scatter_ref):
    flat = got_ref[...].reshape(-1, 2 * BS)
    return pick(scatter_ref[...], flat)


def ridden(got_ref):
    slots = got_ref.shape[1]
    ride = got_ref[0, slots - 1 : slots, :]
    for s in range(1, got_ref.shape[0]):
        ride = ride + got_ref[s, slots - 1 : slots, :]
    return ride


def side_by_side(ref):
    return jnp.concatenate([ref[0], ref[1]], axis=1)


def first_kernel(got_ref, scatter_ref, b_ref, diag_ref, wanted_ref, p_ref, q_ref, out_ref, dots_ref):
    b = side_by_side(b_ref)
    p = arrived(got_ref, scatter_ref) + jnp.concatenate([diag_ref[...]] * 2, axis=1) * b
    p_ref[...] = p
    q_ref[...] = b
    send_out(p, wanted_ref, inner_products(dots_ref, [], b, p, 0), out_ref)


def column_of(ride, j):
    lane = lax.broadcasted_iota(jnp.int32, (1, BS), 1)
    out = []
    for n in range(2):
        row = ride[:, n * BS : (n + 1) * BS]
        inverse = 1.0 / jnp.sqrt(lane_of(row, QQ) + epsilon)
        h = row * jnp.where(lane == j, inverse * inverse, jnp.broadcast_to(inverse, (1, BS)))
        out.append((h, inverse))
    return out


def step_kernel(j, *refs):
    got_ref, scatter_ref, q_ref, p_ref, diag_ref, wanted_ref = refs[:6]
    v_refs = refs[6 : 6 + j]
    m_refs = refs[6 + j : 6 + 2 * j]
    v_ref, m_ref, q_out, p_out, ride_out, out_ref, dots_ref = refs[6 + 2 * j :]
    ride = ridden(got_ref)
    ride_out[...] = jnp.broadcast_to(ride, ride_out.shape)
    coeffs = column_of(ride, j)
    z = arrived(got_ref, scatter_ref)
    for n, (h, inverse) in enumerate(coeffs):
        cut = slice(n * BS, (n + 1) * BS)
        pn = p_ref[:, cut]
        v = q_ref[:, cut] * inverse
        m = pn * inverse
        v_ref[:, cut] = v
        m_ref[:, cut] = m
        q_next = m - lane_of(h, j) * v
        p_next = (z[:, cut] + diag_ref[...] * pn) * inverse - lane_of(h, j) * m
        for i in range(j):
            q_next = q_next - lane_of(h, i) * v_refs[i][:, cut]
            p_next = p_next - lane_of(h, i) * m_refs[i][:, cut]
        q_out[:, cut] = q_next
        p_out[:, cut] = p_next
    p = p_out[...]
    ride = inner_products(dots_ref, [r[...] for r in v_refs] + [v_ref[...]], q_out[...], p, j + 1)
    if j + 1 == STEPS - 1:
        out_ref[...] = jnp.broadcast_to(ride[:, None, :], out_ref.shape)
    else:
        send_out(p, wanted_ref, ride, out_ref)


def finish_kernel(*refs):
    last_ref = refs[0]
    ride_refs = refs[1:STEPS]
    q_ref = refs[STEPS]
    v_refs = refs[STEPS + 1 : 2 * STEPS]
    solution_ref, hessenberg_ref = refs[2 * STEPS :]
    last = jnp.sum(last_ref[...], axis=0)
    rides = [r[0:1, :] for r in ride_refs] + [last]
    per_step = [column_of(ride, j) for j, ride in enumerate(rides)]
    lane = lax.broadcasted_iota(jnp.int32, (1, BS), 1)
    for n in range(2):
        rows = [ride[:, n * BS : (n + 1) * BS] for ride in rides]
        norms = [jnp.sqrt(lane_of(row, QQ) + epsilon) for row in rows]
        columns = [[lane_of(per_step[j][n][0], i) for i in range(j + 1)] for j in range(STEPS)]
        inverses = [per_step[j][n][1] for j in range(STEPS)]
        h = columns[-1]
        remainder = lane_of(rows[-1], PP) * inverses[-1] * inverses[-1]
        for i in range(STEPS):
            remainder = remainder - 2.0 * h[i] * h[i]
            own = lane_of(rows[i], QQ) * inverses[i] * inverses[i]
            remainder = remainder + h[i] * h[i] * own
            for k in range(i):
                gram = lane_of(rows[i], GRAM + k) * inverses[i]
                remainder = remainder + 2.0 * h[i] * h[k] * gram
        final_norm = jnp.sqrt(jnp.maximum(remainder, 0.0) + epsilon)
        below = norms[1:] + [final_norm]
        full = []
        for j in range(STEPS):
            row = jnp.where(lane <= j, per_step[j][n][0], 0.0)
            full.append(jnp.where(lane == j + 1, below[j], row))
        hessenberg_ref[n] = jnp.concatenate(full, axis=0)
        targets = [norms[0]] + [jnp.zeros_like(norms[0])] * STEPS
        cosines, sines, triangle = [], [], []
        for j in range(STEPS):
            rotate(columns[j] + [below[j]], cosines, sines, targets, triangle)
        weights = back_substitute(triangle, targets)
        cut = slice(n * BS, (n + 1) * BS)
        acc = (weights[-1] * inverses[-1]) * q_ref[:, cut]
        for i in range(STEPS - 1):
            acc = acc + weights[i] * v_refs[i][:, cut]
        solution_ref[n] = acc


def slots_of(index, groups, slots, usable):
    places = jnp.arange(groups * BS, dtype=jnp.int32)
    hits = index[:, None] == places[None, :]
    present = hits.any(axis=0).astype(F32).reshape(groups, BS)
    lane = jnp.arange(BS, dtype=jnp.int32)
    before = (lane[:, None] < lane[None, :]).astype(F32)
    rank = jnp.dot(present, before)
    largest = jnp.max(jnp.sum(present, axis=1))
    slot = rank + (jnp.arange(groups, dtype=F32) * slots)[:, None]
    slot_of_block = jnp.sum(jnp.where(hits, slot.reshape(-1)[None, :], 0.0), axis=1)
    wide = jnp.arange(BS, dtype=F32)
    match = (rank[:, None, :] == wide[None, :, None]) & (present[:, None, :] > 0)
    listed = jnp.sum(jnp.where(match, wide[None, None, :] + 1.0, 0.0), axis=2) - 1.0
    listed = jnp.where(wide[None, :] < usable, listed, -1.0)
    return slot_of_block, listed, largest


def body(blocks, block_rows, block_cols, diagonal, right_sides):
    rows_n, cols_n = lax.axis_size(ROW), lax.axis_size(COL)
    count = blocks.shape[0]
    b = right_sides.reshape(2, -1, BS)
    diag = diagonal.reshape(-1, BS)
    block_at = jnp.arange(BS, dtype=F32)

    src_slot, src_list, src_most = slots_of(block_cols[0], rows_n, SRC_SLOTS, SRC_SLOTS - 1)
    asked = swap(jnp.broadcast_to(src_list[:, None, :], (rows_n, 8, BS)), ROW)
    turned = turn_blocks(blocks)
    dst_slot, dst_list, dst_most = slots_of(block_rows[0], cols_n, DST_SLOTS, DST_SLOTS - 1)
    over = ((src_most > SRC_SLOTS - 1) | (dst_most > DST_SLOTS - 1)).astype(F32)
    spread = (src_slot[:, None] == jnp.arange(rows_n * SRC_SLOTS, dtype=F32)[None, :]).astype(BF16)
    sums = (dst_slot[None, :] == jnp.arange(cols_n * DST_SLOTS, dtype=F32)[:, None]).astype(BF16)
    wanted = (asked[:, 0, :SRC_SLOTS].reshape(-1)[:, None] == block_at[None, :]).astype(BF16)
    extra = jnp.concatenate([dst_list, jnp.zeros_like(dst_list)], axis=1)
    lanes = jnp.arange(2 * BS)
    ride = jnp.where(lanes[None, :] == BS + FLAG, over, 0.0) + jnp.zeros((8, 1), F32)

    out_shape = jax.ShapeDtypeStruct((rows_n, SRC_SLOTS, 2 * BS), F32)
    vec = jax.ShapeDtypeStruct((BS, 2 * BS), F32)
    dots = pltpu.VMEM((BS, BS), F32)

    send = call(start_kernel, out_shape, (b, wanted, ride), name="start")
    partial = block_products(swap(send, ROW), spread, turned, sums, extra)
    got = swap(partial, COL)
    last_row = got[:, DST_SLOTS - 1, :]
    overflow = jnp.sum(last_row[:, BS + FLAG])
    scatter = (last_row[:, :DST_SLOTS].reshape(-1)[None, :] == block_at[:, None]).astype(BF16)
    p, q, send = call(first_kernel, (vec, vec, out_shape), (got, scatter, b, diag, wanted), [dots], name="first")
    vs, ms, rides = [], [], []
    for j in range(STEPS - 1):
        got = swap(block_products(swap(send, ROW), spread, turned, sums), COL)
        last = j + 1 == STEPS - 1
        outs = (
            vec, vec, vec, vec, jax.ShapeDtypeStruct((8, 2 * BS), F32),
            jax.ShapeDtypeStruct((rows_n * cols_n, 1, 2 * BS), F32) if last else out_shape,
        )
        v, m, q, p, ride, send = call(
            functools.partial(step_kernel, j), outs, (got, scatter, q, p, diag, wanted, *vs, *ms), [dots],
            name=f"step_{j}",
        )
        vs.append(v)
        ms.append(m)
        rides.append(ride)
    final = swap(send, BOTH)
    solution, hessenberg = call(
        finish_kernel,
        (jax.ShapeDtypeStruct((2, BS, BS), F32), jax.ShapeDtypeStruct((2, STEPS, BS), F32)),
        (final, *rides, q, *vs),
        name="finish",
    )
    solution = solution.reshape(2, -1)
    hessenberg = jnp.swapaxes(hessenberg[:, :, : STEPS + 1], 1, 2)
    return lax.cond(
        overflow > 0.0,
        dense_cycle,
        lambda *unused: (solution, hessenberg),
        blocks, block_rows, block_cols, diagonal, right_sides,
    )


def solution(mesh):
    placed = (P(BOTH, None, None), P(BOTH, None), P(BOTH, None), P(BOTH), P(None, BOTH))
    return jax.shard_map(
        body, mesh=mesh, in_specs=placed, out_specs=(P(None, BOTH), P()), check_vma=False
    )
```

time: 1020 us -> 289 us (0.28)
  matrix products: 273 us -> 0.27 us
  waiting for transfers between devices: 242 us -> 9.01 us
  blocking collectives: 360 us -> 191 us
  Pallas kernels: 0 us -> 48.2 us
  starting transfers between devices: 57.7 us -> 16.2 us
  local copies, waits for them, and re-layouts: 46.8 us -> 13.1 us
  other arithmetic: 30.2 us -> 6.62 us
    dot_general x30 -> x2, matrix products: 273 us -> 0.27 us  [slots_of(): rank = jnp.dot(present, before)]
    psum x36 -> x0, blocking collectives: 242 us -> none  [one_axis_at_a_time(): return functools.reduce(lax.psum, axes, value)]
    all_to_all x11 -> x3, waiting for transfers between devices: 242 us -> 9.01 us  [swap(): return lax.all_to_all(value, axis, split_axis=0, concat_axis=0, tiled=True)]
    all_to_all x5 -> x15, blocking collectives: 117 us -> 191 us  [swap(): return lax.all_to_all(value, axis, split_axis=0, concat_axis=0, tiled=True)]
    pallas_call x0 -> x19, Pallas kernels: none -> 48.2 us  [the longest x18 35.8 us: call(): pl.pallas_call(kernel, out_shape=outs, in_specs=whole(len(operands)), out...]
    all_to_all x11 -> x3, starting transfers between devices: 57.7 us -> 16.2 us  [swap(): return lax.all_to_all(value, axis, split_axis=0, concat_axis=0, tiled=True)]
    another operation x20 -> x0, other arithmetic: 16.6 us -> none
    reshape x8 -> x0, local copies, waits for them, and re-layouts: 10.7 us -> none  [in_blocks(): return jnp.moveaxis(value.reshape(*before, devices, -1, *after), dim, 0)]
  transfers between devices with their start and end apart: 11 -> 3, of which waited for: 11 -> 1; matrix products, arithmetic and copies ran while one was open for 3% -> 2% of each run, Pallas kernels for 0% -> 4%
where the time goes in v1:
time: 289 us; the launch traced here: 288 us
  blocking collectives  191 us (66%)
  Pallas kernels  48.2 us (17%)
  starting transfers between devices  16.2 us (6%)
  local copies, waits for them, and re-layouts  13.1 us (5%)
  waiting for transfers between devices  9.01 us (3%)
  other arithmetic  6.62 us (2%)
  between operations  2.94 us (1%)
    all_to_all x15, blocking collectives, swap(): return lax.all_to_all(value, axis, split_axis=0, concat_axis=0, tiled=True)  191 us
    pallas_call x18, Pallas kernels, call(): pl.pallas_call(kernel, out_shape=outs, in_specs=whole(len(operands)), out...  35.8 us
    all_to_all x3, starting transfers between devices, swap(): return lax.all_to_all(value, axis, split_axis=0, concat_axis=0, tiled=True)  16.2 us
    pallas_call x1, Pallas kernels, turn_blocks(): pl.pallas_call(turn_kernel, out_shape=jax.ShapeDtypeStruct((count // 2, B...  12.4 us
    unnamed x20, local copies, waits for them, and re-layouts  11.6 us
    all_to_all x3, waiting for transfers between devices, swap(): return lax.all_to_all(value, axis, split_axis=0, concat_axis=0, tiled=True)  9.01 us
  transfers between devices with their start and end apart: 3, of which 1 were waited for; matrix products, arithmetic and copies ran while one was open for 2% of the time, Pallas kernels for 4%

profile of v1, /device:TPU:1, one launch (start us, length us, event | category | flops | bytes accessed | tf_op | source)
XLA Modules:
  0.0 287.9 jit_solution(14269531872560221217)
XLA Ops:
  2.6 6.0 %all-to-all-start.2 = ((f32[8,8,128]{2,1,0:T(8,128)}), f32[8,8,128]{2,1,0:T(8,128)S(1)}, u32[]{:S(2)}, u32[]{:S(2)}) async-start(f32[8,8,128]{2,1,0:T(8,128)} %broadcast_in_dim.170), calls=%async_computation.2 | async-start | bytes 65536 | tf_op jit(solution)/shard_map/all_to_all | solution.py:26
  16.6 4.8 %all-to-all-start.3 = ((f32[8,56,256]{2,1,0:T(8,128)}), f32[8,56,256]{2,1,0:T(8,128)S(1)}, u32[]{:S(2)}, u32[]{:S(2)}) async-start(f32[8,56,256]{2,1,0:T(8,128)} %start.1), calls=%async_computation.3 | async-start | bytes 917504 | tf_op jit(solution)/shard_map/all_to_all | solution.py:26
  21.5 12.4 %turn_blocks.1.refs_2_ = bf16[128,128,256]{2,1,0:T(8,128)(2,1)S(1)} custom-call(f32[256,128,128]{2,1,0:T(8,128)} %blocks_ref.1), custom_call_target="tpu_custom_call" | custom-call | tf_op jit(solution)/shard_map/turn_blocks/pallas_call | solution.py:151
  33.8 3.2 %copy-done = bf16[128,128,256]{2,1,0:T(8,128)(2,1)} copy-done((bf16[128,128,256]{2,1,0:T(8,128)(2,1)}, bf16[128,128,256]{2,1,0:T(8,128)(2,1)S(1)}, u32[]{:S(2)}) %copy-start) | copy-done | bytes 8388632
  37.5 3.4 %copy-done.1 = bf16[128,128,256]{2,1,0:T(8,128)(2,1)S(1)} copy-done((bf16[128,128,256]{2,1,0:T(8,128)(2,1)S(1)}, bf16[128,128,256]{2,1,0:T(8,128)(2,1)}, u32[]{:S(2)}) %copy-start.1) | copy-done | bytes 8388632
  43.5 17.0 %all_to_all.118.got_ref = f32[16,24,256]{2,1,0:T(8,128)S(1)} all-to-all(f32[16,24,256]{2,1,0:T(8,128)S(1)} %block_products.8), channel_id=1, replica_groups=mesh['row'=8,'col'=16] {'col'}, dimensions={0} | all-to-all | bytes 786432 | tf_op jit(solution)/shard_map/all_to_all | solution.py:26
  61.7 14.3 %all_to_all.119.refs_0_ = f32[8,56,256]{2,1,0:T(8,128)S(1)} all-to-all(f32[8,56,256]{2,1,0:T(8,128)S(1)} %get-tuple-element.282), channel_id=1, replica_groups=mesh['row'=8,'col'=16] {'row'}, dimensions={0} | all-to-all | bytes 917504 | tf_op jit(solution)/shard_map/all_to_all | solution.py:26
  76.0 3.4 %copy-done.2 = bf16[128,128,256]{2,1,0:T(8,128)(2,1)S(1)} copy-done((bf16[128,128,256]{2,1,0:T(8,128)(2,1)S(1)}, bf16[128,128,256]{2,1,0:T(8,128)(2,1)}, u32[]{:S(2)}) %copy-start.2) | copy-done | bytes 8388632
  82.0 11.6 %all_to_all.120.refs_0_ = f32[16,24,256]{2,1,0:T(8,128)S(1)} all-to-all(f32[16,24,256]{2,1,0:T(8,128)S(1)} %block_products.9), channel_id=1, replica_groups=mesh['row'=8,'col'=16] {'col'}, dimensions={0} | all-to-all | bytes 786432 | tf_op jit(solution)/shard_map/all_to_all | solution.py:26
  94.6 13.2 %all_to_all.121.refs_0_ = f32[8,56,256]{2,1,0:T(8,128)S(1)} all-to-all(f32[8,56,256]{2,1,0:T(8,128)S(1)} %get-tuple-element.285), channel_id=1, replica_groups=mesh['row'=8,'col'=16] {'row'}, dimensions={0} | all-to-all | bytes 917504 | tf_op jit(solution)/shard_map/all_to_all | solution.py:26
  110.4 11.6 %all_to_all.122.refs_0_ = f32[16,24,256]{2,1,0:T(8,128)S(1)} all-to-all(f32[16,24,256]{2,1,0:T(8,128)S(1)} %block_products.10), channel_id=1, replica_groups=mesh['row'=8,'col'=16] {'col'}, dimensions={0} | all-to-all | bytes 786432 | tf_op jit(solution)/shard_map/all_to_all | solution.py:26
  123.0 13.2 %all_to_all.123.refs_0_ = f32[8,56,256]{2,1,0:T(8,128)S(1)} all-to-all(f32[8,56,256]{2,1,0:T(8,128)S(1)} %get-tuple-element.290), channel_id=1, replica_groups=mesh['row'=8,'col'=16] {'row'}, dimensions={0} | all-to-all | bytes 917504 | tf_op jit(solution)/shard_map/all_to_all | solution.py:26
  138.9 11.6 %all_to_all.124.refs_0_ = f32[16,24,256]{2,1,0:T(8,128)S(1)} all-to-all(f32[16,24,256]{2,1,0:T(8,128)S(1)} %block_products.11), channel_id=1, replica_groups=mesh['row'=8,'col'=16] {'col'}, dimensions={0} | all-to-all | bytes 786432 | tf_op jit(solution)/shard_map/all_to_all | solution.py:26
  151.5 13.1 %all_to_all.125.refs_0_ = f32[8,56,256]{2,1,0:T(8,128)S(1)} all-to-all(f32[8,56,256]{2,1,0:T(8,128)S(1)} %get-tuple-element.295), channel_id=1, replica_groups=mesh['row'=8,'col'=16] {'row'}, dimensions={0} | all-to-all | bytes 917504 | tf_op jit(solution)/shard_map/all_to_all | solution.py:26
  167.3 11.6 %all_to_all.126.refs_0_ = f32[16,24,256]{2,1,0:T(8,128)S(1)} all-to-all(f32[16,24,256]{2,1,0:T(8,128)S(1)} %block_products.12), channel_id=1, replica_groups=mesh['row'=8,'col'=16] {'col'}, dimensions={0} | all-to-all | bytes 786432 | tf_op jit(solution)/shard_map/all_to_all | solution.py:26
  180.0 13.2 %all_to_all.127.refs_0_ = f32[8,56,256]{2,1,0:T(8,128)S(1)} all-to-all(f32[8,56,256]{2,1,0:T(8,128)S(1)} %get-tuple-element.300), channel_id=1, replica_groups=mesh['row'=8,'col'=16] {'row'}, dimensions={0} | all-to-all | bytes 917504 | tf_op jit(solution)/shard_map/all_to_all | solution.py:26
  195.9 11.6 %all_to_all.128.refs_0_ = f32[16,24,256]{2,1,0:T(8,128)S(1)} all-to-all(f32[16,24,256]{2,1,0:T(8,128)S(1)} %block_products.13), channel_id=1, replica_groups=mesh['row'=8,'col'=16] {'col'}, dimensions={0} | all-to-all | bytes 786432 | tf_op jit(solution)/shard_map/all_to_all | solution.py:26
  208.6 13.1 %all_to_all.129.refs_0_ = f32[8,56,256]{2,1,0:T(8,128)S(1)} all-to-all(f32[8,56,256]{2,1,0:T(8,128)S(1)} %get-tuple-element.305), channel_id=1, replica_groups=mesh['row'=8,'col'=16] {'row'}, dimensions={0} | all-to-all | bytes 917504 | tf_op jit(solution)/shard_map/all_to_all | solution.py:26
  224.4 11.6 %all_to_all.130.refs_0_ = f32[16,24,256]{2,1,0:T(8,128)S(1)} all-to-all(f32[16,24,256]{2,1,0:T(8,128)S(1)} %block_products.14), channel_id=1, replica_groups=mesh['row'=8,'col'=16] {'col'}, dimensions={0} | all-to-all | bytes 786432 | tf_op jit(solution)/shard_map/all_to_all | solution.py:26
  237.2 13.2 %all_to_all.131.refs_0_ = f32[8,56,256]{2,1,0:T(8,128)S(1)} all-to-all(f32[8,56,256]{2,1,0:T(8,128)S(1)} %get-tuple-element.310), channel_id=1, replica_groups=mesh['row'=8,'col'=16] {'row'}, dimensions={0} | all-to-all | bytes 917504 | tf_op jit(solution)/shard_map/all_to_all | solution.py:26
  253.0 11.6 %all_to_all.132.refs_0_ = f32[16,24,256]{2,1,0:T(8,128)S(1)} all-to-all(f32[16,24,256]{2,1,0:T(8,128)S(1)} %block_products.15), channel_id=1, replica_groups=mesh['row'=8,'col'=16] {'col'}, dimensions={0} | all-to-all | bytes 786432 | tf_op jit(solution)/shard_map/all_to_all | solution.py:26
  266.2 5.5 %all-to-all-start.19 = ((f32[128,1,256]{2,1,0:T(1,128)}), f32[128,1,256]{2,1,0:T(1,128)S(1)}, u32[]{:S(2)}, u32[]{:S(2)}) async-start(f32[128,1,256]{2,1,0:T(1,128)} %get-tuple-element.315), calls=%async_computation.19 | async-start | bytes 262144 | tf_op jit(solution)/shard_map/all_to_all | solution.py:26
  273.0 9.0 %all-to-all-done.19.refs_0_ = f32[128,1,256]{2,1,0:T(1,128)S(1)} async-done(((f32[128,1,256]{2,1,0:T(1,128)}), f32[128,1,256]{2,1,0:T(1,128)S(1)}, u32[]{:S(2)}, u32[]{:S(2)}) %all-to-all-start.19) | async-done | bytes 131104 | tf_op jit(solution)/shard_map/all_to_all | solution.py:26
  282.0 4.2 %finish.1 = (f32[2,128,128]{2,1,0:T(8,128)S(1)}, f32[2,8,128]{2,1,0:T(8,128)S(1)}) custom-call(f32[128,1,256]{2,1,0:T(1,128)S(1)} %all-to-all-done.19.refs_0_, f32[8,256]{1,0:T(8,128)S(1)} %get-tuple-element.316.refs_1_, f32[8,256]{1,0:T(8,128)S(1)} %get-tuple-element.317.refs_2_, f32[8,256]{1,0:T(8,128)S(1)} %get-tuple-element.318.refs_3_, ...), custom_call_target="tpu_custom_call" | custom-call | tf_op jit(solution)/shard_map/finish/pallas_call | solution.py:119
  (76 shorter events, 42.0 us)
Async XLA Ops:
  2.6 12.6 %all-to-all-start.2 = ((f32[8,8,128]{2,1,0:T(8,128)}), f32[8,8,128]{2,1,0:T(8,128)S(1)}, u32[]{:S(2)}, u32[]{:S(2)}) async-start(f32[8,8,128]{2,1,0:T(8,128)} %broadcast_in_dim.170), calls=%async_computation.2 | async-start | bytes 65536 | tf_op jit(solution)/shard_map/all_to_all | solution.py:26
  16.6 20.9 %all-to-all-start.3 = ((f32[8,56,256]{2,1,0:T(8,128)}), f32[8,56,256]{2,1,0:T(8,128)S(1)}, u32[]{:S(2)}, u32[]{:S(2)}) async-start(f32[8,56,256]{2,1,0:T(8,128)} %start.1), calls=%async_computation.3 | async-start | bytes 917504 | tf_op jit(solution)/shard_map/all_to_all | solution.py:26
  21.5 15.6 %copy-start.7 = (s32[1,256]{1,0:T(1,128)S(1)}, s32[1,256]{1,0:T(1,128)}, u32[]{:S(2)}) copy-start(s32[1,256]{1,0:T(1,128)} %param.15) | copy-start | bytes 3076
  33.8 3.2 %copy-start = (bf16[128,128,256]{2,1,0:T(8,128)(2,1)}, bf16[128,128,256]{2,1,0:T(8,128)(2,1)S(1)}, u32[]{:S(2)}) copy-start(bf16[128,128,256]{2,1,0:T(8,128)(2,1)S(1)} %turn_blocks.1.refs_2_) | copy-start | bytes 25165828
  37.4 3.4 %copy-start.1 = (bf16[128,128,256]{2,1,0:T(8,128)(2,1)S(1)}, bf16[128,128,256]{2,1,0:T(8,128)(2,1)}, u32[]{:S(2)}) copy-start(bf16[128,128,256]{2,1,0:T(8,128)(2,1)} %copy-done) | copy-start | bytes 25165828
  40.8 19.9 %copy-start.4 = (f32[16384]{0:T(1024)S(1)}, f32[16384]{0:T(1024)}, u32[]{:S(2)}) copy-start(f32[16384]{0:T(1024)} %param.16) | copy-start | bytes 196612
  76.0 3.4 %copy-start.2 = (bf16[128,128,256]{2,1,0:T(8,128)(2,1)S(1)}, bf16[128,128,256]{2,1,0:T(8,128)(2,1)}, u32[]{:S(2)}) copy-start(bf16[128,128,256]{2,1,0:T(8,128)(2,1)} %copy-done) | copy-start | bytes 25165828
  79.4 28.4 %copy-start.3 = (bf16[128,128,256]{2,1,0:T(8,128)(2,1)S(1)}, bf16[128,128,256]{2,1,0:T(8,128)(2,1)}, u32[]{:S(2)}) copy-start(bf16[128,128,256]{2,1,0:T(8,128)(2,1)} %copy-done) | copy-start | bytes 25165828
  264.6 22.2 %copy-start.5 = (f32[2,16384]{1,0:T(2,128)S(1)}, f32[2,16384]{1,0:T(2,128)}, u32[]{:S(2)}) copy-start(f32[2,16384]{1,0:T(2,128)} %param.17) | copy-start | bytes 393220
  264.6 22.2 %copy-start.8 = (s32[1,256]{1,0:T(1,128)S(1)}, s32[1,256]{1,0:T(1,128)}, u32[]{:S(2)}) copy-start(s32[1,256]{1,0:T(1,128)} %param.14) | copy-start | bytes 3076
  266.2 15.8 %all-to-all-start.19 = ((f32[128,1,256]{2,1,0:T(1,128)}), f32[128,1,256]{2,1,0:T(1,128)S(1)}, u32[]{:S(2)}, u32[]{:S(2)}) async-start(f32[128,1,256]{2,1,0:T(1,128)} %get-tuple-element.315), calls=%async_computation.19 | async-start | bytes 262144 | tf_op jit(solution)/shard_map/all_to_all | solution.py:26
  287.2 0.7 copy-start.6

commit v2 on v1

v2 whole, which is shorter than its diff:
```python
import functools

import jax
import jax.numpy as jnp
from jax import lax
from jax.experimental import pallas as pl
from jax.experimental.pallas import tpu as pltpu
from jax.sharding import PartitionSpec as P

STEPS = 8
BS = 128
SRC_SLOTS = 56
DST_SLOTS = 24
ROW = "row"
COL = "col"
BOTH = ("row", "col")
F32 = jnp.float32
BF16 = jnp.bfloat16

epsilon = 1e-06

QQ, PP, GRAM, FLAG = 9, 10, 16, 127


def swap(value, axis):
    return lax.all_to_all(value, axis, split_axis=0, concat_axis=0, tiled=True)


def least_squares(hessenberg, initial_norm):
    total_steps = hessenberg.shape[2]
    targets = [initial_norm] + [jnp.zeros_like(initial_norm) for j in range(total_steps)]
    cosines, sines, triangle = ([], [], [])
    for j in range(total_steps):
        column = [hessenberg[:, i, j] for i in range(j + 2)]
        rotate(column, cosines, sines, targets, triangle)
    return jnp.stack(back_substitute(triangle, targets), axis=1)


def rotate(column, cosines, sines, targets, triangle):
    j = len(column) - 2
    for i in range(j):
        leading, trailing = (column[i], column[i + 1])
        column[i] = cosines[i] * leading + sines[i] * trailing
        column[i + 1] = cosines[i] * trailing - sines[i] * leading
    radius = jnp.sqrt(column[j] * column[j] + column[j + 1] * column[j + 1])
    cosine = column[j] / radius
    sine_term = column[j + 1] / radius
    column[j] = radius
    cosines.append(cosine)
    sines.append(sine_term)
    targets[j + 1] = -sine_term * targets[j]
    targets[j] = cosine * targets[j]
    triangle.append(column[: j + 1])


def back_substitute(triangle, targets):
    total_steps = len(triangle)
    coeffs = [None] * total_steps
    for j in reversed(range(total_steps)):
        running = targets[j]
        for k in range(j + 1, total_steps):
            running = running - triangle[k][j] * coeffs[k]
        coeffs[j] = running / triangle[j][j]
    return coeffs


def dense_cycle(blocks, block_rows, block_cols, diagonal, right_sides):
    systems = right_sides.shape[0]
    groups = lax.axis_size(COL)
    length = right_sides.shape[1]
    row_count = groups * (length // BS)
    positions = jnp.arange(row_count, dtype=jnp.int32)
    onehot = (block_rows[0][None, :] == positions[:, None]).astype(F32)
    high = lax.Precision.HIGHEST

    def everywhere(value):
        return lax.psum(lax.psum(value, ROW), COL)

    def apply_matrix(vector):
        copies = jnp.broadcast_to(vector, (lax.axis_size(ROW), *vector.shape))
        gathered = jnp.moveaxis(swap(copies, ROW), 0, 1).reshape(systems, -1, BS)
        picked = jnp.take(gathered, block_cols[0], axis=1)
        products = jnp.sum(blocks[None] * picked[:, :, None, :], axis=3)
        partial = jnp.einsum("mk,nki->mni", onehot, products, precision=high)
        own = swap(partial.reshape(groups, -1, systems, BS), COL).sum(axis=0)
        return diagonal[None, :] * vector + jnp.transpose(own, (1, 0, 2)).reshape(systems, -1)

    def norm(vector):
        return jnp.sqrt(everywhere(jnp.sum(vector * vector, axis=1)) + epsilon)

    initial_norm = norm(right_sides)
    basis = jnp.zeros((STEPS + 1, systems, length), F32).at[0].set(right_sides / initial_norm[:, None])
    hessenberg = jnp.zeros((systems, STEPS + 1, STEPS), F32)

    def step(j, state):
        basis, hessenberg = state
        candidate = apply_matrix(basis[j])
        coeffs = everywhere(jnp.sum(basis * candidate[None], axis=2).T)
        candidate = candidate - jnp.sum(coeffs.T[:, :, None] * basis, axis=0)
        new_norm = norm(candidate)
        below = (jnp.arange(STEPS + 1) == j + 1).astype(F32)
        column = coeffs + below[None, :] * new_norm[:, None]
        here = (jnp.arange(STEPS) == j).astype(F32)
        hessenberg = hessenberg + column[:, :, None] * here[None, None, :]
        basis = basis.at[j + 1].set(candidate / new_norm[:, None])
        return basis, hessenberg

    basis, hessenberg = lax.fori_loop(0, STEPS, step, (basis, hessenberg))
    weights = least_squares(hessenberg, initial_norm)
    solution = jnp.sum(weights.T[:, :, None] * basis[:STEPS], axis=0)
    return solution, hessenberg


def whole(count):
    return [pl.BlockSpec(memory_space=pltpu.VMEM)] * count


def call(kernel, outs, operands, scratch=(), vmem=24 << 20, name=None):
    return pl.pallas_call(
        kernel,
        out_shape=outs,
        in_specs=whole(len(operands)),
        out_specs=jax.tree.map(lambda o: pl.BlockSpec(memory_space=pltpu.VMEM), outs),
        scratch_shapes=list(scratch),
        compiler_params=pltpu.CompilerParams(vmem_limit_bytes=vmem),
        name=name,
    )(*operands)


def pieces(value, count):
    out = []
    for _ in range(count):
        piece = value.astype(BF16)
        out.append(piece)
        value = value - piece.astype(F32)
    return out


def pick(selector, value, count=3):
    return sum(jnp.dot(selector, piece, preferred_element_type=F32) for piece in pieces(value, count))


PER_CHUNK = 16
AHEAD = 6


def turned_pair(read):
    return jnp.concatenate([read(half).astype(BF16).T for half in range(2)], axis=1)


def gather_sources(got_ref, spread_ref, left_ref):
    sources, slots = got_ref.shape[0], got_ref.shape[1]
    got = got_ref[...].reshape(sources * slots, 2 * BS)
    count = spread_ref.shape[0]
    for at, piece in enumerate(pieces(got, 2)):
        picked = jnp.dot(spread_ref[...], piece, preferred_element_type=F32)
        left_ref[pl.ds(2 * at, count, stride=4), :] = picked[:, :BS]
        left_ref[pl.ds(2 * at + 1, count, stride=4), :] = picked[:, BS:]


def multiply_pair(rows, turned, left_ref, prod_ref):
    upper = lax.broadcasted_iota(jnp.int32, (8, BS), 0) < 4
    both = jnp.dot(left_ref[rows, :].astype(BF16), turned, preferred_element_type=F32)
    prod_ref[rows, :] = jnp.where(upper, both[:, :BS], both[:, BS:])


def sum_targets(prod_ref, sums_ref, out_ref):
    count = sums_ref.shape[1]
    products = jnp.concatenate(
        [prod_ref[pl.ds(n, count, stride=4), :] + prod_ref[pl.ds(n + 2, count, stride=4), :] for n in range(2)],
        axis=1,
    )
    out_ref[...] = pick(sums_ref[...], products).reshape(out_ref.shape)


def first_product_kernel(
    got_ref, spread_ref, blocks_ref, sums_ref, lists_ref, out_ref, turned_ref, left_ref, prod_ref, held_ref, sem
):
    chunks, per_chunk = held_ref.shape[0], held_ref.shape[1]
    pairs = per_chunk // 2

    def fetch(chunk):
        start = pl.multiple_of(chunk * per_chunk, per_chunk)
        return pltpu.make_async_copy(blocks_ref.at[pl.ds(start, per_chunk)], held_ref.at[chunk], sem.at[chunk])

    for chunk in range(AHEAD):
        fetch(chunk).start()
    gather_sources(got_ref, spread_ref, left_ref)

    def one(chunk, carry):
        fetch(chunk).wait()

        @pl.when(chunk + AHEAD < chunks)
        def _():
            fetch(chunk + AHEAD).start()

        for pair in range(pairs):
            turned = turned_pair(lambda half: held_ref[chunk, 2 * pair + half])
            at = chunk * pairs + pair
            turned_ref[at] = turned
            multiply_pair(pl.ds(pl.multiple_of(8 * at, 8), 8), turned, left_ref, prod_ref)
        return carry

    lax.fori_loop(0, chunks, one, 0)
    sum_targets(prod_ref, sums_ref, out_ref)
    targets, slots = out_ref.shape[0], out_ref.shape[1]
    for t in range(targets):
        out_ref[t, slots - 1 : slots, :] = lists_ref[...].astype(F32) - float(t * BS)


def product_kernel(got_ref, spread_ref, turned_ref, sums_ref, out_ref, left_ref, prod_ref):
    gather_sources(got_ref, spread_ref, left_ref)
    for pair in range(turned_ref.shape[0]):
        multiply_pair(slice(8 * pair, 8 * pair + 8), turned_ref[pair], left_ref, prod_ref)
    sum_targets(prod_ref, sums_ref, out_ref)
    slots = out_ref.shape[1]
    ride = ridden(got_ref)
    for t in range(out_ref.shape[0]):
        out_ref[t, slots - 1 : slots, :] = ride


def first_products(got, spread, blocks, sums, lists):
    count = spread.shape[0]
    targets = sums.shape[0] // DST_SLOTS
    chunks = count // PER_CHUNK
    specs = whole(5)
    specs[2] = pl.BlockSpec(memory_space=pltpu.HBM)
    return pl.pallas_call(
        first_product_kernel,
        out_shape=(
            jax.ShapeDtypeStruct((targets, DST_SLOTS, 2 * BS), F32),
            jax.ShapeDtypeStruct((count // 2, BS, 2 * BS), BF16),
        ),
        in_specs=specs,
        out_specs=(pl.BlockSpec(memory_space=pltpu.VMEM), pl.BlockSpec(memory_space=pltpu.VMEM)),
        scratch_shapes=[
            pltpu.VMEM((4 * count, BS), F32),
            pltpu.VMEM((4 * count, BS), F32),
            pltpu.VMEM((chunks, PER_CHUNK, BS, BS), F32),
            pltpu.SemaphoreType.DMA((chunks,)),
        ],
        compiler_params=pltpu.CompilerParams(vmem_limit_bytes=32 << 20),
        name="first_products",
    )(got, spread, blocks, sums, lists)


def block_products(got, spread, turned, sums):
    count = spread.shape[0]
    targets = sums.shape[0] // DST_SLOTS
    return call(
        product_kernel,
        jax.ShapeDtypeStruct((targets, DST_SLOTS, 2 * BS), F32),
        (got, spread, turned, sums),
        [pltpu.VMEM((4 * count, BS), F32), pltpu.VMEM((4 * count, BS), F32)],
        vmem=16 << 20,
        name="block_products",
    )


def lane_of(row, lane):
    return row[:, lane : lane + 1]


def total(value):
    return jnp.sum(value, axis=0, keepdims=True)


def send_out(values, wanted_ref, ride, out_ref):
    out = pick(wanted_ref[...], values)
    out_ref[...] = out.reshape(out_ref.shape)
    slots = out_ref.shape[1]
    for s in range(out_ref.shape[0]):
        out_ref[s, slots - 1 : slots, :] = ride


def ranks(present):
    shape = (BS, BS)
    before = lax.broadcasted_iota(jnp.int32, shape, 0) < lax.broadcasted_iota(jnp.int32, shape, 1)
    return jnp.dot(present.astype(BF16), before.astype(F32).astype(BF16), preferred_element_type=F32)


def present_in(column, offset):
    lane = lax.broadcasted_iota(jnp.int32, (column.shape[0], BS), 1).astype(F32) + offset
    return jnp.max(jnp.where(column == lane, 1.0, 0.0), axis=0, keepdims=True)


def slot_rows(present, rank, slots, usable):
    at = lax.broadcasted_iota(jnp.int32, (slots, BS), 0).astype(F32)
    return jnp.where((rank == at) & (present > 0.0) & (at < usable), 1.0, 0.0)


def one_hots(lists, slots):
    columns = lists.T
    present = jnp.concatenate([present_in(columns[:, g : g + 1], 0.0) for g in range(lists.shape[0])], axis=0)
    rank = ranks(present)
    return jnp.concatenate(
        [slot_rows(present[g : g + 1], rank[g : g + 1], slots, slots - 1.0) for g in range(lists.shape[0])], axis=0
    )


def slot_column(index, groups, slots):
    column = jnp.broadcast_to(index, (8, index.shape[1])).T[:, :1]
    present = jnp.concatenate([present_in(column, float(g * BS)) for g in range(groups)], axis=0)
    rank = ranks(present)
    lane = lax.broadcasted_iota(jnp.int32, (column.shape[0], BS), 1).astype(F32)
    found = jnp.zeros(lane.shape, F32)
    for g in range(groups):
        found = found + jnp.where(column == lane + float(g * BS), rank[g : g + 1] + float(g * slots), 0.0)
    largest = jnp.max(jnp.sum(present, axis=1, keepdims=True), axis=0, keepdims=True)
    return jnp.sum(found, axis=1, keepdims=True), largest


def plan_kernel(sources, targets, cols_ref, rows_ref, spread_ref, sums_ref, over_ref):
    count = cols_ref.shape[1]
    column, src_most = slot_column(cols_ref[...].astype(F32), sources, SRC_SLOTS)
    at = lax.broadcasted_iota(jnp.int32, spread_ref.shape, 1).astype(F32)
    spread_ref[...] = jnp.where(column == at, 1.0, 0.0).astype(BF16)
    column, dst_most = slot_column(rows_ref[...].astype(F32), targets, DST_SLOTS)
    row = jnp.broadcast_to(column, (count, BS)).T[:1, :]
    at = lax.broadcasted_iota(jnp.int32, sums_ref.shape, 0).astype(F32)
    sums_ref[...] = jnp.where(row == at, 1.0, 0.0).astype(BF16)
    over = jnp.where((src_most > SRC_SLOTS - 1.0) | (dst_most > DST_SLOTS - 1.0), 1.0, 0.0)
    lane = lax.broadcasted_iota(jnp.int32, over_ref.shape, 1)
    over_ref[...] = jnp.where(lane == BS + FLAG, over, 0.0)


def start_kernel(asked_ref, b_ref, wanted_ref, out_ref):
    lists = jnp.concatenate([asked_ref[g, 0:1, :] for g in range(asked_ref.shape[0])], axis=0)
    wanted_ref[...] = one_hots(lists, SRC_SLOTS).astype(BF16)
    send_out(side_by_side(b_ref), wanted_ref, jnp.zeros((1, 2 * BS), F32), out_ref)


def inner_products(dots_ref, vs, q, p, j):
    rides = []
    for n in range(2):
        cut = slice(n * BS, (n + 1) * BS)
        dots_ref[...] = jnp.zeros(dots_ref.shape, F32)
        qn, pn = q[:, cut], p[:, cut]
        for i in range(j):
            vn = vs[i][:, cut]
            dots_ref[i : i + 1, :] = total(vn * pn)
            dots_ref[GRAM + i : GRAM + i + 1, :] = total(vn * qn)
        dots_ref[j : j + 1, :] = total(qn * pn)
        dots_ref[QQ : QQ + 1, :] = total(qn * qn)
        dots_ref[PP : PP + 1, :] = total(pn * pn)
        ones = jnp.ones((8, BS), F32)
        row = lax.dot_general(
            ones, dots_ref[...], (((1,), (1,)), ((), ())),
            precision=lax.Precision.HIGHEST, preferred_element_type=F32,
        )
        rides.append(row[0:1, :])
    return jnp.concatenate(rides, axis=1)


def arrived(got_ref, scatter_ref):
    flat = got_ref[...].reshape(-1, 2 * BS)
    return pick(scatter_ref[...], flat)


def ridden(got_ref):
    slots = got_ref.shape[1]
    ride = got_ref[0, slots - 1 : slots, :]
    for s in range(1, got_ref.shape[0]):
        ride = ride + got_ref[s, slots - 1 : slots, :]
    return ride


def side_by_side(ref):
    return jnp.concatenate([ref[0], ref[1]], axis=1)


def first_kernel(got_ref, over_ref, b_ref, diag_ref, wanted_ref, scatter_ref, p_ref, q_ref, out_ref, dots_ref):
    slots = got_ref.shape[1]
    lists = jnp.concatenate([got_ref[g, slots - 1 : slots, :] for g in range(got_ref.shape[0])], axis=0)
    scatter_ref[...] = one_hots(lists, DST_SLOTS).T.astype(BF16)
    b = side_by_side(b_ref)
    p = arrived(got_ref, scatter_ref) + jnp.concatenate([diag_ref[...]] * 2, axis=1) * b
    p_ref[...] = p
    q_ref[...] = b
    send_out(p, wanted_ref, inner_products(dots_ref, [], b, p, 0) + over_ref[0:1, :], out_ref)


def column_of(ride, j):
    lane = lax.broadcasted_iota(jnp.int32, (1, BS), 1)
    out = []
    for n in range(2):
        row = ride[:, n * BS : (n + 1) * BS]
        inverse = 1.0 / jnp.sqrt(lane_of(row, QQ) + epsilon)
        h = row * jnp.where(lane == j, inverse * inverse, jnp.broadcast_to(inverse, (1, BS)))
        out.append((h, inverse))
    return out


def step_kernel(j, *refs):
    got_ref, scatter_ref, q_ref, p_ref, diag_ref, wanted_ref = refs[:6]
    v_refs = refs[6 : 6 + j]
    m_refs = refs[6 + j : 6 + 2 * j]
    v_ref, m_ref, q_out, p_out, ride_out, out_ref, dots_ref = refs[6 + 2 * j :]
    ride = ridden(got_ref)
    ride_out[...] = jnp.broadcast_to(ride, ride_out.shape)
    coeffs = column_of(ride, j)
    z = arrived(got_ref, scatter_ref)
    for n, (h, inverse) in enumerate(coeffs):
        cut = slice(n * BS, (n + 1) * BS)
        pn = p_ref[:, cut]
        v = q_ref[:, cut] * inverse
        m = pn * inverse
        v_ref[:, cut] = v
        m_ref[:, cut] = m
        q_next = m - lane_of(h, j) * v
        p_next = (z[:, cut] + diag_ref[...] * pn) * inverse - lane_of(h, j) * m
        for i in range(j):
            q_next = q_next - lane_of(h, i) * v_refs[i][:, cut]
            p_next = p_next - lane_of(h, i) * m_refs[i][:, cut]
        q_out[:, cut] = q_next
        p_out[:, cut] = p_next
    p = p_out[...]
    ride = inner_products(dots_ref, [r[...] for r in v_refs] + [v_ref[...]], q_out[...], p, j + 1)
    if j + 1 == STEPS - 1:
        out_ref[...] = jnp.broadcast_to(ride[:, None, :], out_ref.shape)
    else:
        send_out(p, wanted_ref, ride, out_ref)


GRAM_AT, NUMBERS_AT = 16, 24
KEPT_ROWS = 96


def rotations_kernel(*refs):
    ride_refs, kept_ref = refs[:-1], refs[-1]
    rides = [r[0:1, :] for r in ride_refs]
    per_step = [column_of(ride, j) for j, ride in enumerate(rides)]
    lane = lax.broadcasted_iota(jnp.int32, (1, BS), 1)
    known = len(rides)
    kept_ref[...] = jnp.zeros(kept_ref.shape, F32)
    for n in range(2):
        rows = [ride[:, n * BS : (n + 1) * BS] for ride in rides]
        norms = [jnp.sqrt(lane_of(row, QQ) + epsilon) for row in rows]
        inverses = [per_step[j][n][1] for j in range(known)]
        for j in range(known):
            column = jnp.where(lane <= j, per_step[j][n][0], 0.0)
            if j + 1 < known:
                column = jnp.where(lane == j + 1, norms[j + 1], column)
            kept_ref[n, j : j + 1, :] = column
            gram = pltpu.roll(rows[j], BS - GRAM, 1) * inverses[j]
            own = lane_of(rows[j], QQ) * inverses[j] * inverses[j]
            gram = jnp.where(lane < j, 2.0 * gram, 0.0)
            kept_ref[n, GRAM_AT + j : GRAM_AT + j + 1, :] = jnp.where(lane == j, own, gram)
        targets = [norms[0]] + [jnp.zeros_like(norms[0])] * known
        cosines, sines, triangle = [], [], []
        for j in range(known - 1):
            column = [lane_of(per_step[j][n][0], i) for i in range(j + 1)]
            rotate(column + [norms[j + 1]], cosines, sines, targets, triangle)
        numbers = cosines + sines + [x for column in triangle for x in column] + targets[:known]
        for at, number in enumerate(numbers):
            kept_ref[n, NUMBERS_AT + at : NUMBERS_AT + at + 1, :] = jnp.broadcast_to(number, (1, BS))


def finish_kernel(last_ref, kept_ref, q_ref, *refs):
    v_refs, (solution_ref, hessenberg_ref) = refs[:-2], refs[-2:]
    known = STEPS - 1
    ride = jnp.sum(last_ref[...], axis=0)
    lane = lax.broadcasted_iota(jnp.int32, (1, BS), 1)
    both = []
    for n, (h, inverse) in enumerate(column_of(ride, known)):
        row = ride[:, n * BS : (n + 1) * BS]
        norm = jnp.sqrt(lane_of(row, QQ) + epsilon)
        h = jnp.where(lane <= known, h, 0.0)
        gram = jnp.where(lane < known, 2.0 * pltpu.roll(row, BS - GRAM, 1) * inverse, 0.0)
        gram = jnp.where(lane == known, lane_of(row, QQ) * inverse * inverse, gram)
        table = jnp.concatenate([kept_ref[n, GRAM_AT : GRAM_AT + known, :], gram], axis=0)
        column = jnp.broadcast_to(h, (8, BS)).T[:8, :1]
        form = jnp.sum(jnp.sum(table * h * column, axis=1, keepdims=True), axis=0, keepdims=True)
        twice = 2.0 * jnp.sum(h * h, axis=1, keepdims=True)
        remainder = lane_of(row, PP) * inverse * inverse - twice + form
        final_norm = jnp.sqrt(jnp.maximum(remainder, 0.0) + epsilon)
        columns = jnp.concatenate([kept_ref[n, :known, :], jnp.where(lane == known + 1, final_norm, h)], axis=0)
        before_last = lax.broadcasted_iota(jnp.int32, columns.shape, 0) == known - 1
        columns = jnp.where(before_last & (lane == known), norm, columns)
        hessenberg_ref[n] = columns.T[: STEPS + 1, :]

        def number(at):
            return kept_ref[n, NUMBERS_AT + at : NUMBERS_AT + at + 1, :]

        cosines = [number(i) for i in range(known - 1)]
        sines = [number(known - 1 + i) for i in range(known - 1)]
        at, triangle = 2 * (known - 1), []
        for j in range(known - 1):
            triangle.append([number(at + i) for i in range(j + 1)])
            at += j + 1
        targets = [number(at + i) for i in range(known)] + [None, None]
        wide = jnp.zeros((1, BS), F32)
        previous = kept_ref[n, known - 1 : known, :]
        column = [wide + lane_of(previous, i) for i in range(known)] + [wide + norm]
        rotate(column, cosines, sines, targets, triangle)
        column = [wide + lane_of(h, i) for i in range(STEPS)] + [wide + final_norm]
        rotate(column, cosines, sines, targets, triangle)
        weights = back_substitute(triangle, targets)
        cut = slice(n * BS, (n + 1) * BS)
        acc = (weights[-1] * inverse) * q_ref[:, cut]
        for i in range(STEPS - 1):
            acc = acc + weights[i] * v_refs[i][:, cut]
        both.append(acc)
    for block in range(BS):
        row = jnp.concatenate([acc[block : block + 1, :] for acc in both], axis=0)
        solution_ref[:, block * BS : (block + 1) * BS] = row


def body(blocks, block_rows, block_cols, diagonal, right_sides):
    rows_n, cols_n = lax.axis_size(ROW), lax.axis_size(COL)
    count = blocks.shape[0]
    b = right_sides.reshape(2, -1, BS)
    diag = diagonal.reshape(-1, BS)

    group = jnp.arange(rows_n, dtype=jnp.int32)[:, None, None]
    relative = (block_cols[None] - group * BS).astype(F32)
    asked = swap(jnp.broadcast_to(relative, (rows_n, 8, count)), ROW)
    spread, sums, over = call(
        functools.partial(plan_kernel, rows_n, cols_n),
        (
            jax.ShapeDtypeStruct((count, rows_n * SRC_SLOTS), BF16),
            jax.ShapeDtypeStruct((cols_n * DST_SLOTS, count), BF16),
            jax.ShapeDtypeStruct((8, 2 * BS), F32),
        ),
        (block_cols, block_rows),
        name="plan",
    )

    out_shape = jax.ShapeDtypeStruct((rows_n, SRC_SLOTS, 2 * BS), F32)
    vec = jax.ShapeDtypeStruct((BS, 2 * BS), F32)
    dots = pltpu.VMEM((BS, BS), F32)

    wanted, send = call(
        start_kernel, (jax.ShapeDtypeStruct((rows_n * SRC_SLOTS, BS), BF16), out_shape), (asked, b), name="start"
    )
    partial, turned = first_products(swap(send, ROW), spread, blocks, sums, block_rows)
    got = swap(partial, COL)
    scatter, p, q, send = call(
        first_kernel,
        (jax.ShapeDtypeStruct((BS, cols_n * DST_SLOTS), BF16), vec, vec, out_shape),
        (got, over, b, diag, wanted),
        [dots],
        name="first",
    )
    vs, ms, rides = [], [], []
    for j in range(STEPS - 1):
        got = swap(block_products(swap(send, ROW), spread, turned, sums), COL)
        last = j + 1 == STEPS - 1
        outs = (
            vec, vec, vec, vec, jax.ShapeDtypeStruct((8, 2 * BS), F32),
            jax.ShapeDtypeStruct((rows_n * cols_n, 1, 2 * BS), F32) if last else out_shape,
        )
        v, m, q, p, ride, send = call(
            functools.partial(step_kernel, j), outs, (got, scatter, q, p, diag, wanted, *vs, *ms), [dots],
            name=f"step_{j}",
        )
        vs.append(v)
        ms.append(m)
        rides.append(ride)
    final = swap(send, BOTH)
    so_far = call(
        rotations_kernel, jax.ShapeDtypeStruct((2, KEPT_ROWS, BS), F32), tuple(rides), name="rotations"
    )

    def compact(final, so_far, q, *vs):
        solution, hessenberg = call(
            finish_kernel,
            (
                jax.ShapeDtypeStruct((2, BS * BS), F32),
                jax.ShapeDtypeStruct((2, STEPS + 1, STEPS), F32),
            ),
            (final, so_far, q, *vs),
            name="finish",
        )
        return solution, hessenberg

    return lax.cond(
        rides[0][0, BS + FLAG] > 0.0,
        lambda *args: dense_cycle(*args[:5]),
        lambda *args: compact(*args[5:]),
        blocks, block_rows, block_cols, diagonal, right_sides, final, so_far, q, *vs,
    )


def solution(mesh):
    placed = (P(BOTH, None, None), P(BOTH, None), P(BOTH, None), P(BOTH), P(None, BOTH))
    return jax.shard_map(
        body, mesh=mesh, in_specs=placed, out_specs=(P(None, BOTH), P()), check_vma=False
    )
```

time: 289 us -> 266 us (0.920)
  Pallas kernels: 48.2 us -> 35.7 us
  local copies, waits for them, and re-layouts: 13.1 us -> 2.83 us
  waiting for transfers between devices: 9.01 us -> 18.8 us
  other arithmetic: 6.62 us -> 0.8 us
    unnamed x20 -> x9, local copies, waits for them, and re-layouts: 11.6 us -> 0.93 us
    all_to_all x3, waiting for transfers between devices: 9.01 us -> 18.8 us  [swap(): return lax.all_to_all(value, axis, split_axis=0, concat_axis=0, tiled=True)]
    pallas_call x18 -> x19, Pallas kernels: 35.8 us -> 28.8 us  [call(): pl.pallas_call(kernel, out_shape=outs, in_specs=whole(len(operands)), out...]
    pallas_call x1, Pallas kernels: 12.4 us -> 6.91 us  [first_products(): pl.pallas_call(first_product_kernel, out_shape=(jax.ShapeDtypeStruct((tar...]
  transfers between devices with their start and end apart: 3 -> 3, of which waited for: 1 -> 3; matrix products, arithmetic and copies ran while one was open for 2% -> 1% of each run, Pallas kernels for 4% -> 1%
where the time goes in v2:
time: 266 us; the launch traced here: 265 us
  blocking collectives  190 us (71%)
  Pallas kernels  35.7 us (13%)
  waiting for transfers between devices  18.8 us (7%)
  starting transfers between devices  15.6 us (6%)
  local copies, waits for them, and re-layouts  2.83 us (1%)
    all_to_all x15, blocking collectives, swap(): return lax.all_to_all(value, axis, split_axis=0, concat_axis=0, tiled=True)  190 us
    pallas_call x19, Pallas kernels, call(): pl.pallas_call(kernel, out_shape=outs, in_specs=whole(len(operands)), out...  28.8 us
    all_to_all x3, waiting for transfers between devices, swap(): return lax.all_to_all(value, axis, split_axis=0, concat_axis=0, tiled=True)  18.8 us
    all_to_all x3, starting transfers between devices, swap(): return lax.all_to_all(value, axis, split_axis=0, concat_axis=0, tiled=True)  15.6 us
    pallas_call x1, Pallas kernels, first_products(): pl.pallas_call(first_product_kernel, out_shape=(jax.ShapeDtypeStruct((tar...  6.91 us
  transfers between devices with their start and end apart: 3, of which 3 were waited for; matrix products, arithmetic and copies ran while one was open for 1% of the time, Pallas kernels for 1%

profile of v2, /device:TPU:1, one launch (start us, length us, event | category | flops | bytes accessed | tf_op | source)
XLA Modules:
  0.0 264.8 jit_solution(4069111161234196457)
XLA Ops:
  2.1 6.0 %all-to-all-start.2 = ((f32[8,8,256]{2,1,0:T(8,128)}), f32[8,8,256]{2,1,0:T(8,128)S(1)}, u32[]{:S(2)}, u32[]{:S(2)}) async-start(f32[8,8,256]{2,1,0:T(8,128)} %broadcast_in_dim.67), calls=%async_computation.2 | async-start | bytes 131072 | tf_op jit(solution)/shard_map/all_to_all | solution.py:26
  9.0 3.9 %all-to-all-done.2.asked_ref = f32[8,8,256]{2,1,0:T(8,128)S(1)} async-done(((f32[8,8,256]{2,1,0:T(8,128)}), f32[8,8,256]{2,1,0:T(8,128)S(1)}, u32[]{:S(2)}, u32[]{:S(2)}) %all-to-all-start.2) | async-done | bytes 65568 | tf_op jit(solution)/shard_map/all_to_all | solution.py:26
  14.7 4.2 %all-to-all-start.3 = ((f32[8,56,256]{2,1,0:T(8,128)}), f32[8,56,256]{2,1,0:T(8,128)S(1)}, u32[]{:S(2)}, u32[]{:S(2)}) async-start(f32[8,56,256]{2,1,0:T(8,128)} %get-tuple-element.309), calls=%async_computation.3 | async-start | bytes 917504 | tf_op jit(solution)/shard_map/all_to_all | solution.py:26
  20.2 7.3 %all-to-all-done.3.got_ref = f32[8,56,256]{2,1,0:T(8,128)S(1)} async-done(((f32[8,56,256]{2,1,0:T(8,128)}), f32[8,56,256]{2,1,0:T(8,128)S(1)}, u32[]{:S(2)}, u32[]{:S(2)}) %all-to-all-start.3) | async-done | bytes 458784 | tf_op jit(solution)/shard_map/all_to_all | solution.py:26
  27.5 6.9 %first_products.1 = (f32[16,24,256]{2,1,0:T(8,128)S(1)}, bf16[128,128,256]{2,1,0:T(8,128)(2,1)S(1)}) custom-call(f32[8,56,256]{2,1,0:T(8,128)S(1)} %all-to-all-done.3.got_ref, bf16[256,448]{1,0:T(8,128)(2,1)S(1)} %get-tuple-element.310.spread_ref, f32[256,128,128]{2,1,0:T(8,128)} %blocks_ref.1, bf16[384,256]{1,0:T(8,128)(2,1)S(1)} %get-tuple-element.311.sums_ref, ...), custom_call_target="tpu_custom_call" | custom-call | tf_op jit(solution)/shard_map/first_products/pallas_call | solution.py:228
  34.5 16.3 %all_to_all.118.got_ref = f32[16,24,256]{2,1,0:T(8,128)S(1)} all-to-all(f32[16,24,256]{2,1,0:T(8,128)S(1)} %get-tuple-element.312), channel_id=1, replica_groups=mesh['row'=8,'col'=16] {'col'}, dimensions={0} | all-to-all | bytes 786432 | tf_op jit(solution)/shard_map/all_to_all | solution.py:26
  50.8 1.9 first.1
  52.7 13.2 %all_to_all.119.got_ref = f32[8,56,256]{2,1,0:T(8,128)S(1)} all-to-all(f32[8,56,256]{2,1,0:T(8,128)S(1)} %get-tuple-element.315), channel_id=1, replica_groups=mesh['row'=8,'col'=16] {'row'}, dimensions={0} | all-to-all | bytes 917504 | tf_op jit(solution)/shard_map/all_to_all | solution.py:26
  67.7 11.6 %all_to_all.120.refs_0_ = f32[16,24,256]{2,1,0:T(8,128)S(1)} all-to-all(f32[16,24,256]{2,1,0:T(8,128)S(1)} %block_products.7), channel_id=1, replica_groups=mesh['row'=8,'col'=16] {'col'}, dimensions={0} | all-to-all | bytes 786432 | tf_op jit(solution)/shard_map/all_to_all | solution.py:26
  80.3 13.2 %all_to_all.121.got_ref = f32[8,56,256]{2,1,0:T(8,128)S(1)} all-to-all(f32[8,56,256]{2,1,0:T(8,128)S(1)} %get-tuple-element.321), channel_id=1, replica_groups=mesh['row'=8,'col'=16] {'row'}, dimensions={0} | all-to-all | bytes 917504 | tf_op jit(solution)/shard_map/all_to_all | solution.py:26
  95.3 11.6 %all_to_all.122.refs_0_ = f32[16,24,256]{2,1,0:T(8,128)S(1)} all-to-all(f32[16,24,256]{2,1,0:T(8,128)S(1)} %block_products.8), channel_id=1, replica_groups=mesh['row'=8,'col'=16] {'col'}, dimensions={0} | all-to-all | bytes 786432 | tf_op jit(solution)/shard_map/all_to_all | solution.py:26
  107.9 13.1 %all_to_all.123.got_ref = f32[8,56,256]{2,1,0:T(8,128)S(1)} all-to-all(f32[8,56,256]{2,1,0:T(8,128)S(1)} %get-tuple-element.326), channel_id=1, replica_groups=mesh['row'=8,'col'=16] {'row'}, dimensions={0} | all-to-all | bytes 917504 | tf_op jit(solution)/shard_map/all_to_all | solution.py:26
  122.9 11.6 %all_to_all.124.refs_0_ = f32[16,24,256]{2,1,0:T(8,128)S(1)} all-to-all(f32[16,24,256]{2,1,0:T(8,128)S(1)} %block_products.9), channel_id=1, replica_groups=mesh['row'=8,'col'=16] {'col'}, dimensions={0} | all-to-all | bytes 786432 | tf_op jit(solution)/shard_map/all_to_all | solution.py:26
  135.5 13.3 %all_to_all.125.got_ref = f32[8,56,256]{2,1,0:T(8,128)S(1)} all-to-all(f32[8,56,256]{2,1,0:T(8,128)S(1)} %get-tuple-element.331), channel_id=1, replica_groups=mesh['row'=8,'col'=16] {'row'}, dimensions={0} | all-to-all | bytes 917504 | tf_op jit(solution)/shard_map/all_to_all | solution.py:26
  150.7 11.6 %all_to_all.126.refs_0_ = f32[16,24,256]{2,1,0:T(8,128)S(1)} all-to-all(f32[16,24,256]{2,1,0:T(8,128)S(1)} %block_products.10), channel_id=1, replica_groups=mesh['row'=8,'col'=16] {'col'}, dimensions={0} | all-to-all | bytes 786432 | tf_op jit(solution)/shard_map/all_to_all | solution.py:26
  163.4 13.1 %all_to_all.127.got_ref = f32[8,56,256]{2,1,0:T(8,128)S(1)} all-to-all(f32[8,56,256]{2,1,0:T(8,128)S(1)} %get-tuple-element.336), channel_id=1, replica_groups=mesh['row'=8,'col'=16] {'row'}, dimensions={0} | all-to-all | bytes 917504 | tf_op jit(solution)/shard_map/all_to_all | solution.py:26
  178.3 11.6 %all_to_all.128.refs_0_ = f32[16,24,256]{2,1,0:T(8,128)S(1)} all-to-all(f32[16,24,256]{2,1,0:T(8,128)S(1)} %block_products.11), channel_id=1, replica_groups=mesh['row'=8,'col'=16] {'col'}, dimensions={0} | all-to-all | bytes 786432 | tf_op jit(solution)/shard_map/all_to_all | solution.py:26
  191.1 13.2 %all_to_all.129.got_ref = f32[8,56,256]{2,1,0:T(8,128)S(1)} all-to-all(f32[8,56,256]{2,1,0:T(8,128)S(1)} %get-tuple-element.341), channel_id=1, replica_groups=mesh['row'=8,'col'=16] {'row'}, dimensions={0} | all-to-all | bytes 917504 | tf_op jit(solution)/shard_map/all_to_all | solution.py:26
  206.0 11.6 %all_to_all.130.refs_0_ = f32[16,24,256]{2,1,0:T(8,128)S(1)} all-to-all(f32[16,24,256]{2,1,0:T(8,128)S(1)} %block_products.12), channel_id=1, replica_groups=mesh['row'=8,'col'=16] {'col'}, dimensions={0} | all-to-all | bytes 786432 | tf_op jit(solution)/shard_map/all_to_all | solution.py:26
  218.8 13.1 %all_to_all.131.got_ref = f32[8,56,256]{2,1,0:T(8,128)S(1)} all-to-all(f32[8,56,256]{2,1,0:T(8,128)S(1)} %get-tuple-element.346), channel_id=1, replica_groups=mesh['row'=8,'col'=16] {'row'}, dimensions={0} | all-to-all | bytes 917504 | tf_op jit(solution)/shard_map/all_to_all | solution.py:26
  233.8 11.6 %all_to_all.132.refs_0_ = f32[16,24,256]{2,1,0:T(8,128)S(1)} all-to-all(f32[16,24,256]{2,1,0:T(8,128)S(1)} %block_products.13), channel_id=1, replica_groups=mesh['row'=8,'col'=16] {'col'}, dimensions={0} | all-to-all | bytes 786432 | tf_op jit(solution)/shard_map/all_to_all | solution.py:26
  246.9 5.5 %all-to-all-start.19 = ((f32[128,1,256]{2,1,0:T(1,128)}), f32[128,1,256]{2,1,0:T(1,128)S(1)}, u32[]{:S(2)}, u32[]{:S(2)}) async-start(f32[128,1,256]{2,1,0:T(1,128)} %get-tuple-element.351), calls=%async_computation.19 | async-start | bytes 262144 | tf_op jit(solution)/shard_map/all_to_all | solution.py:26
  255.1 7.6 %all-to-all-done.19 = f32[128,1,256]{2,1,0:T(1,128)S(1)} async-done(((f32[128,1,256]{2,1,0:T(1,128)}), f32[128,1,256]{2,1,0:T(1,128)S(1)}, u32[]{:S(2)}, u32[]{:S(2)}) %all-to-all-start.19) | async-done | bytes 131104 | tf_op jit(solution)/shard_map/all_to_all | solution.py:26
  262.8 2.1 conditional.1
  (32 shorter events, 30.5 us)
Async XLA Ops:
  0.6 18.2 %copy-start.5 = (s32[1,256]{1,0:T(1,128)S(1)}, s32[1,256]{1,0:T(1,128)}, u32[]{:S(2)}) copy-start(s32[1,256]{1,0:T(1,128)} %cols_ref.1) | copy-start | bytes 3076
  0.6 18.2 %copy-start.4 = (s32[1,256]{1,0:T(1,128)S(1)}, s32[1,256]{1,0:T(1,128)}, u32[]{:S(2)}) copy-start(s32[1,256]{1,0:T(1,128)} %lists_ref.1) | copy-start | bytes 3076
  2.1 10.8 %all-to-all-start.2 = ((f32[8,8,256]{2,1,0:T(8,128)}), f32[8,8,256]{2,1,0:T(8,128)S(1)}, u32[]{:S(2)}, u32[]{:S(2)}) async-start(f32[8,8,256]{2,1,0:T(8,128)} %broadcast_in_dim.67), calls=%async_computation.2 | async-start | bytes 131072 | tf_op jit(solution)/shard_map/all_to_all | solution.py:26
  14.7 12.8 %all-to-all-start.3 = ((f32[8,56,256]{2,1,0:T(8,128)}), f32[8,56,256]{2,1,0:T(8,128)S(1)}, u32[]{:S(2)}, u32[]{:S(2)}) async-start(f32[8,56,256]{2,1,0:T(8,128)} %get-tuple-element.309), calls=%async_computation.3 | async-start | bytes 917504 | tf_op jit(solution)/shard_map/all_to_all | solution.py:26
  27.5 23.3 %copy-start = (f32[16384]{0:T(1024)S(1)}, f32[16384]{0:T(1024)}, u32[]{:S(2)}) copy-start(f32[16384]{0:T(1024)} %param.16) | copy-start | bytes 196612
  245.3 17.4 %copy-start.2 = (f32[2,16384]{1,0:T(2,128)S(1)}, f32[2,16384]{1,0:T(2,128)}, u32[]{:S(2)}) copy-start(f32[2,16384]{1,0:T(2,128)} %param.17) | copy-start | bytes 393220
  246.9 15.8 %all-to-all-start.19 = ((f32[128,1,256]{2,1,0:T(1,128)}), f32[128,1,256]{2,1,0:T(1,128)S(1)}, u32[]{:S(2)}, u32[]{:S(2)}) async-start(f32[128,1,256]{2,1,0:T(1,128)} %get-tuple-element.351), calls=%async_computation.19 | async-start | bytes 262144 | tf_op jit(solution)/shard_map/all_to_all | solution.py:26

commit v3 on v2

--- a/solution.py
+++ b/solution.py
@@ -140,12 +140,62 @@
     return sum(jnp.dot(selector, piece, preferred_element_type=F32) for piece in pieces(value, count))
 
 
-PER_CHUNK = 16
-AHEAD = 6
-
-
-def turned_pair(read):
-    return jnp.concatenate([read(half).astype(BF16).T for half in range(2)], axis=1)
+CHUNKS = 8
+
+
+def turn_kernel(blocks_ref, turned_ref, held_ref, made_ref, arrived_sem, left_sem):
+    steps, per_step = held_ref.shape[0], held_ref.shape[1]
+    pairs = per_step // 2
+
+    def fetch(step):
+        return pltpu.make_async_copy(
+            blocks_ref.at[pl.ds(pl.multiple_of(step * per_step, per_step), per_step)],
+            held_ref.at[step],
+            arrived_sem.at[step],
+        )
+
+    def keep(step):
+        return pltpu.make_async_copy(
+            made_ref.at[step],
+            turned_ref.at[pl.ds(pl.multiple_of(step * pairs, pairs), pairs)],
+            left_sem.at[step],
+        )
+
+    for step in range(steps):
+        fetch(step).start()
+
+    def one(step, carry):
+        fetch(step).wait()
+        for pair in range(pairs):
+            made_ref[step, pair] = jnp.concatenate(
+                [held_ref[step, 2 * pair + half].astype(BF16).T for half in range(2)], axis=1
+            )
+        keep(step).start()
+        return carry
+
+    lax.fori_loop(0, steps, one, 0)
+    for step in range(steps):
+        keep(step).wait()
+
+
+def turn_blocks(blocks, per_step=16):
+    count = blocks.shape[0]
+    steps = count // per_step
+    return pl.pallas_call(
+        turn_kernel,
+        out_shape=pltpu.MemorySpace.HBM((count // 2, BS, 2 * BS), BF16),
+        in_specs=[pl.BlockSpec(memory_space=pltpu.HBM)],
+        out_specs=pl.BlockSpec(memory_space=pltpu.HBM),
+        scratch_shapes=[
+            pltpu.VMEM((steps, per_step, BS, BS), F32),
+            pltpu.VMEM((steps, per_step // 2, BS, 2 * BS), BF16),
+            pltpu.SemaphoreType.DMA((steps,)),
+            pltpu.SemaphoreType.DMA((steps,)),
+        ],
+        compiler_params=pltpu.CompilerParams(vmem_limit_bytes=28 << 20),
+        cost_estimate=pl.CostEstimate(flops=40_000_000, transcendentals=0, bytes_accessed=count * BS * BS * 6),
+        name="turn_blocks",
+    )(blocks)
 
 
 def gather_sources(got_ref, spread_ref, left_ref):
@@ -174,44 +224,44 @@
 
 
 def first_product_kernel(
-    got_ref, spread_ref, blocks_ref, sums_ref, lists_ref, out_ref, turned_ref, left_ref, prod_ref, held_ref, sem
+    got_ref, spread_ref, stored_ref, sums_ref, lists_ref, out_ref, turned_ref, wanted_ref, left_ref, prod_ref, sem
 ):
-    chunks, per_chunk = held_ref.shape[0], held_ref.shape[1]
-    pairs = per_chunk // 2
+    per_chunk = stored_ref.shape[0] // CHUNKS
 
     def fetch(chunk):
-        start = pl.multiple_of(chunk * per_chunk, per_chunk)
-        return pltpu.make_async_copy(blocks_ref.at[pl.ds(start, per_chunk)], held_ref.at[chunk], sem.at[chunk])
-
-    for chunk in range(AHEAD):
+        where = pl.ds(pl.multiple_of(chunk * per_chunk, per_chunk), per_chunk)
+        return pltpu.make_async_copy(stored_ref.at[where], turned_ref.at[where], sem.at[chunk])
+
+    for chunk in range(CHUNKS):
         fetch(chunk).start()
     gather_sources(got_ref, spread_ref, left_ref)
+    asked = jnp.concatenate([got_ref[g, BS : BS + 1, :] for g in range(got_ref.shape[0])], axis=0)
+    wanted_ref[...] = one_hots(asked, SRC_SLOTS).astype(BF16)
 
     def one(chunk, carry):
         fetch(chunk).wait()
-
-        @pl.when(chunk + AHEAD < chunks)
-        def _():
-            fetch(chunk + AHEAD).start()
-
-        for pair in range(pairs):
-            turned = turned_pair(lambda half: held_ref[chunk, 2 * pair + half])
-            at = chunk * pairs + pair
-            turned_ref[at] = turned
-            multiply_pair(pl.ds(pl.multiple_of(8 * at, 8), 8), turned, left_ref, prod_ref)
+        for k in range(per_chunk):
+            pair = chunk * per_chunk + k
+            multiply_pair(pl.ds(pl.multiple_of(8 * pair, 8), 8), turned_ref[pair], left_ref, prod_ref)
         return carry
 
-    lax.fori_loop(0, chunks, one, 0)
+    lax.fori_loop(0, CHUNKS, one, 0)
     sum_targets(prod_ref, sums_ref, out_ref)
     targets, slots = out_ref.shape[0], out_ref.shape[1]
+    lists = lists_ref[0:1, :]
     for t in range(targets):
-        out_ref[t, slots - 1 : slots, :] = lists_ref[...].astype(F32) - float(t * BS)
+        own = pltpu.roll(lists, lists.shape[1] - t * slots, 1) if t else lists
+        out_ref[t, slots - 1 : slots, :] = own[:, : 2 * BS]
 
 
 def product_kernel(got_ref, spread_ref, turned_ref, sums_ref, out_ref, left_ref, prod_ref):
     gather_sources(got_ref, spread_ref, left_ref)
-    for pair in range(turned_ref.shape[0]):
-        multiply_pair(slice(8 * pair, 8 * pair + 8), turned_ref[pair], left_ref, prod_ref)
+
+    def one(pair, carry):
+        multiply_pair(pl.ds(pl.multiple_of(8 * pair, 8), 8), turned_ref[pair], left_ref, prod_ref)
+        return carry
+
+    lax.fori_loop(0, turned_ref.shape[0], one, 0, unroll=64)
     sum_targets(prod_ref, sums_ref, out_ref)
     slots = out_ref.shape[1]
     ride = ridden(got_ref)
@@ -219,29 +269,30 @@
         out_ref[t, slots - 1 : slots, :] = ride
 
 
-def first_products(got, spread, blocks, sums, lists):
+def first_products(got, spread, stored, sums, lists):
     count = spread.shape[0]
+    sources = got.shape[0]
     targets = sums.shape[0] // DST_SLOTS
-    chunks = count // PER_CHUNK
     specs = whole(5)
     specs[2] = pl.BlockSpec(memory_space=pltpu.HBM)
+    outs = (
+        jax.ShapeDtypeStruct((targets, DST_SLOTS, 2 * BS), F32),
+        jax.ShapeDtypeStruct(stored.shape, BF16),
+        jax.ShapeDtypeStruct((sources * SRC_SLOTS, BS), BF16),
+    )
     return pl.pallas_call(
         first_product_kernel,
-        out_shape=(
-            jax.ShapeDtypeStruct((targets, DST_SLOTS, 2 * BS), F32),
-            jax.ShapeDtypeStruct((count // 2, BS, 2 * BS), BF16),
-        ),
+        out_shape=outs,
         in_specs=specs,
-        out_specs=(pl.BlockSpec(memory_space=pltpu.VMEM), pl.BlockSpec(memory_space=pltpu.VMEM)),
+        out_specs=tuple(whole(3)),
         scratch_shapes=[
             pltpu.VMEM((4 * count, BS), F32),
             pltpu.VMEM((4 * count, BS), F32),
-            pltpu.VMEM((chunks, PER_CHUNK, BS, BS), F32),
-            pltpu.SemaphoreType.DMA((chunks,)),
+            pltpu.SemaphoreType.DMA((CHUNKS,)),
         ],
-        compiler_params=pltpu.CompilerParams(vmem_limit_bytes=32 << 20),
+        compiler_params=pltpu.CompilerParams(vmem_limit_bytes=24 << 20),
         name="first_products",
-    )(got, spread, blocks, sums, lists)
+    )(got, spread, pltpu.with_memory_space_constraint(stored, pltpu.HBM), sums, lists)
 
 
 def block_products(got, spread, turned, sums):
@@ -298,36 +349,67 @@
     )
 
 
-def slot_column(index, groups, slots):
-    column = jnp.broadcast_to(index, (8, index.shape[1])).T[:, :1]
-    present = jnp.concatenate([present_in(column, float(g * BS)) for g in range(groups)], axis=0)
-    rank = ranks(present)
-    lane = lax.broadcasted_iota(jnp.int32, (column.shape[0], BS), 1).astype(F32)
-    found = jnp.zeros(lane.shape, F32)
-    for g in range(groups):
-        found = found + jnp.where(column == lane + float(g * BS), rank[g : g + 1] + float(g * slots), 0.0)
-    largest = jnp.max(jnp.sum(present, axis=1, keepdims=True), axis=0, keepdims=True)
-    return jnp.sum(found, axis=1, keepdims=True), largest
-
-
-def plan_kernel(sources, targets, cols_ref, rows_ref, spread_ref, sums_ref, over_ref):
+def plan_kernel(sources, targets, cols_ref, rows_ref, whole_ref, spread_ref, sums_ref, lists_ref, over_ref):
     count = cols_ref.shape[1]
-    column, src_most = slot_column(cols_ref[...].astype(F32), sources, SRC_SLOTS)
+
+    def column_of_blocks(ref):
+        return jnp.broadcast_to(ref[...].astype(F32), (8, count)).T[:, :1]
+
+    def present_and_rank(column, groups):
+        present = jnp.concatenate([present_in(column, float(g * BS)) for g in range(groups)], axis=0)
+        return present, ranks(present)
+
+    def slot_column(column, rank, groups, slots):
+        lane = lax.broadcasted_iota(jnp.int32, (count, BS), 1).astype(F32)
+        found = jnp.zeros(lane.shape, F32)
+        for g in range(groups):
+            found = found + jnp.where(column == lane + float(g * BS), rank[g : g + 1] + float(g * slots), 0.0)
+        return jnp.sum(found, axis=1, keepdims=True)
+
+    def most(present):
+        return jnp.max(jnp.sum(present, axis=1, keepdims=True), axis=0, keepdims=True)
+
+    column = column_of_blocks(cols_ref)
+    present, rank = present_and_rank(column, sources)
+    slot = slot_column(column, rank, sources, SRC_SLOTS)
     at = lax.broadcasted_iota(jnp.int32, spread_ref.shape, 1).astype(F32)
-    spread_ref[...] = jnp.where(column == at, 1.0, 0.0).astype(BF16)
-    column, dst_most = slot_column(rows_ref[...].astype(F32), targets, DST_SLOTS)
-    row = jnp.broadcast_to(column, (count, BS)).T[:1, :]
+    spread_ref[...] = jnp.where(slot == at, 1.0, 0.0).astype(BF16)
+    pitch = whole_ref.shape[1] // sources
+    at = lax.broadcasted_iota(jnp.int32, (count, pitch), 1).astype(F32)
+    in_group = jnp.concatenate(
+        [jnp.where((column - float(g * BS) == at) & (at < BS), 1.0, 0.0) for g in range(sources)], axis=1
+    )
+    whole_ref[...] = in_group.astype(BF16)
+    over = most(present) > SRC_SLOTS - 1.0
+
+    column = column_of_blocks(rows_ref)
+    present, rank = present_and_rank(column, targets)
+    slot = slot_column(column, rank, targets, DST_SLOTS)
+    row = jnp.broadcast_to(slot, (count, BS)).T[:1, :]
     at = lax.broadcasted_iota(jnp.int32, sums_ref.shape, 0).astype(F32)
     sums_ref[...] = jnp.where(row == at, 1.0, 0.0).astype(BF16)
-    over = jnp.where((src_most > SRC_SLOTS - 1.0) | (dst_most > DST_SLOTS - 1.0), 1.0, 0.0)
+    listed = jnp.concatenate(
+        [slot_rows(present[t : t + 1], rank[t : t + 1], DST_SLOTS, DST_SLOTS - 1.0) for t in range(targets)], axis=0
+    )
+    number = lax.broadcasted_iota(jnp.int32, (8, BS), 1).astype(F32) + 1.0
+    lists_ref[...] = lax.dot_general(
+        number.astype(BF16), listed.astype(BF16), (((1,), (1,)), ((), ())), preferred_element_type=F32
+    ) - 1.0
+    over = jnp.where(over | (most(present) > DST_SLOTS - 1.0), 1.0, 0.0)
     lane = lax.broadcasted_iota(jnp.int32, over_ref.shape, 1)
     over_ref[...] = jnp.where(lane == BS + FLAG, over, 0.0)
 
 
-def start_kernel(asked_ref, b_ref, wanted_ref, out_ref):
-    lists = jnp.concatenate([asked_ref[g, 0:1, :] for g in range(asked_ref.shape[0])], axis=0)
-    wanted_ref[...] = one_hots(lists, SRC_SLOTS).astype(BF16)
-    send_out(side_by_side(b_ref), wanted_ref, jnp.zeros((1, 2 * BS), F32), out_ref)
+def open_kernel(sides_ref, cols_ref, out_ref, b_ref):
+    for at in range(0, BS, 8):
+        tiles = [sides_ref[:, (at + k) * BS : (at + k + 1) * BS] for k in range(8)]
+        for n in range(2):
+            b_ref[at : at + 8, n * BS : (n + 1) * BS] = jnp.concatenate([t[n : n + 1, :] for t in tiles], axis=0)
+    below = lax.broadcasted_iota(jnp.int32, (8, 2 * BS), 0) == 0
+    cols = cols_ref[...].astype(F32)
+    for g in range(out_ref.shape[0]):
+        out_ref[g, :BS, :] = b_ref[...]
+        out_ref[g, BS:, :] = jnp.where(below, cols - float(g * BS), 0.0)
 
 
 def inner_products(dots_ref, vs, q, p, j):
@@ -365,18 +447,15 @@
     return ride
 
 
-def side_by_side(ref):
-    return jnp.concatenate([ref[0], ref[1]], axis=1)
-
-
-def first_kernel(got_ref, over_ref, b_ref, diag_ref, wanted_ref, scatter_ref, p_ref, q_ref, out_ref, dots_ref):
-    slots = got_ref.shape[1]
-    lists = jnp.concatenate([got_ref[g, slots - 1 : slots, :] for g in range(got_ref.shape[0])], axis=0)
-    scatter_ref[...] = one_hots(lists, DST_SLOTS).T.astype(BF16)
-    b = side_by_side(b_ref)
+def first_kernel(got_ref, over_ref, b_ref, diag_ref, wanted_ref, scatter_ref, p_ref, out_ref, dots_ref):
+    sources, slots = got_ref.shape[0], got_ref.shape[1]
+    lists = jnp.concatenate([got_ref[g, slots - 1 : slots, :BS] for g in range(sources)], axis=0).T
+    lane = lax.broadcasted_iota(jnp.int32, (slots, BS), 1).astype(F32)
+    rows = [jnp.where(lists[:slots, g : g + 1] == lane, 1.0, 0.0) for g in range(sources)]
+    scatter_ref[...] = jnp.concatenate(rows, axis=0).T.astype(BF16)
+    b = b_ref[...]
     p = arrived(got_ref, scatter_ref) + jnp.concatenate([diag_ref[...]] * 2, axis=1) * b
     p_ref[...] = p
-    q_ref[...] = b
     send_out(p, wanted_ref, inner_products(dots_ref, [], b, p, 0) + over_ref[0:1, :], out_ref)
 
 
@@ -509,17 +588,24 @@
 def body(blocks, block_rows, block_cols, diagonal, right_sides):
     rows_n, cols_n = lax.axis_size(ROW), lax.axis_size(COL)
     count = blocks.shape[0]
-    b = right_sides.reshape(2, -1, BS)
     diag = diagonal.reshape(-1, BS)
-
-    group = jnp.arange(rows_n, dtype=jnp.int32)[:, None, None]
-    relative = (block_cols[None] - group * BS).astype(F32)
-    asked = swap(jnp.broadcast_to(relative, (rows_n, 8, count)), ROW)
-    spread, sums, over = call(
+    pitch = BS + 8
+
+    pieces_out, q = call(
+        open_kernel,
+        (jax.ShapeDtypeStruct((rows_n, pitch, 2 * BS), F32), jax.ShapeDtypeStruct((BS, 2 * BS), F32)),
+        (right_sides, block_cols),
+        name="open",
+    )
+    got = swap(pieces_out, ROW)
+    stored = turn_blocks(blocks)
+    from_whole, spread, sums, lists, over = call(
         functools.partial(plan_kernel, rows_n, cols_n),
         (
+            jax.ShapeDtypeStruct((count, rows_n * pitch), BF16),
             jax.ShapeDtypeStruct((count, rows_n * SRC_SLOTS), BF16),
             jax.ShapeDtypeStruct((cols_n * DST_SLOTS, count), BF16),
+            jax.ShapeDtypeStruct((8, cols_n * DST_SLOTS), F32),
             jax.ShapeDtypeStruct((8, 2 * BS), F32),
         ),
         (block_cols, block_rows),
@@ -530,15 +616,12 @@
     vec = jax.ShapeDtypeStruct((BS, 2 * BS), F32)
     dots = pltpu.VMEM((BS, BS), F32)
 
-    wanted, send = call(
-        start_kernel, (jax.ShapeDtypeStruct((rows_n * SRC_SLOTS, BS), BF16), out_shape), (asked, b), name="start"
-    )
-    partial, turned = first_products(swap(send, ROW), spread, blocks, sums, block_rows)
+    partial, turned, wanted = first_products(got, from_whole, stored, sums, lists)
     got = swap(partial, COL)
-    scatter, p, q, send = call(
+    scatter, p, send = call(
         first_kernel,
-        (jax.ShapeDtypeStruct((BS, cols_n * DST_SLOTS), BF16), vec, vec, out_shape),
-        (got, over, b, diag, wanted),
+        (jax.ShapeDtypeStruct((BS, cols_n * DST_SLOTS), BF16), vec, out_shape),
+        (got, over, q, diag, wanted),
         [dots],
         name="first",
     )

time: 266 us -> 260 us (0.977)
  Pallas kernels: 35.7 us -> 43.8 us
  waiting for transfers between devices: 18.8 us -> 11.7 us
  starting transfers between devices: 15.6 us -> 11.5 us
    all_to_all x3 -> x2, waiting for transfers between devices: 18.8 us -> 11.7 us  [swap(): return lax.all_to_all(value, axis, split_axis=0, concat_axis=0, tiled=True)]
    pallas_call x1 -> x2, Pallas kernels: 6.91 us -> 13.7 us  [the longest x1 9.53 us: turn_blocks(): pl.pallas_call(turn_kernel, out_shape=pltpu.MemorySpace.HBM((count // 2,...]
    all_to_all x3 -> x2, starting transfers between devices: 15.6 us -> 11.5 us  [swap(): return lax.all_to_all(value, axis, split_axis=0, concat_axis=0, tiled=True)]
  transfers between devices with their start and end apart: 3 -> 2, of which waited for: 3 -> 2; matrix products, arithmetic and copies ran while one was open for 1% -> 0% of each run, Pallas kernels for 1% -> 5%
where the time goes in v3:
time: 260 us; the launch traced here: 259 us
  blocking collectives  189 us (73%)
  Pallas kernels  43.8 us (17%)
  waiting for transfers between devices  11.7 us (4%)
  starting transfers between devices  11.5 us (4%)
    all_to_all x15, blocking collectives, swap(): return lax.all_to_all(value, axis, split_axis=0, concat_axis=0, tiled=True)  189 us
    pallas_call x19, Pallas kernels, call(): pl.pallas_call(kernel, out_shape=outs, in_specs=whole(len(operands)), out...  30.1 us
    all_to_all x2, waiting for transfers between devices, swap(): return lax.all_to_all(value, axis, split_axis=0, concat_axis=0, tiled=True)  11.7 us
    all_to_all x2, starting transfers between devices, swap(): return lax.all_to_all(value, axis, split_axis=0, concat_axis=0, tiled=True)  11.5 us
    pallas_call x1, Pallas kernels, turn_blocks(): pl.pallas_call(turn_kernel, out_shape=pltpu.MemorySpace.HBM((count // 2,...  9.53 us
  transfers between devices with their start and end apart: 2, of which 2 were waited for; matrix products, arithmetic and copies ran while one was open for 0% of the time, Pallas kernels for 5%

profile of v3, /device:TPU:1, one launch (start us, length us, event | category | flops | bytes accessed | tf_op | source)
XLA Modules:
  0.0 259.1 jit_solution(14833130820485152179)
XLA Ops:
  0.6 2.1 open.1
  2.8 6.0 %all-to-all-start.2 = ((f32[8,136,256]{2,1,0:T(8,128)}), f32[8,136,256]{2,1,0:T(8,128)S(1)}, u32[]{:S(2)}, u32[]{:S(2)}) async-start(f32[8,136,256]{2,1,0:T(8,128)} %get-tuple-element.311), calls=%async_computation.2 | async-start | bytes 2228224 | tf_op jit(solution)/shard_map/all_to_all | solution.py:26
  8.7 2.1 plan.1
  10.8 9.5 %turn_blocks.1.stored_ref = bf16[128,128,256]{2,1,0:T(8,128)(2,1)} custom-call(f32[256,128,128]{2,1,0:T(8,128)} %blocks_ref.1), custom_call_target="tpu_custom_call" | custom-call | flops 40000000 | bytes 25165824 | tf_op jit(solution)/shard_map/turn_blocks/pallas_call | solution.py:184
  20.3 4.1 %all-to-all-done.2.got_ref = f32[8,136,256]{2,1,0:T(8,128)S(1)} async-done(((f32[8,136,256]{2,1,0:T(8,128)}), f32[8,136,256]{2,1,0:T(8,128)S(1)}, u32[]{:S(2)}, u32[]{:S(2)}) %all-to-all-start.2) | async-done | bytes 1114144 | tf_op jit(solution)/shard_map/all_to_all | solution.py:26
  24.4 4.2 %first_products.1 = (f32[16,24,256]{2,1,0:T(8,128)S(1)}, bf16[128,128,256]{2,1,0:T(8,128)(2,1)S(1)}, bf16[448,128]{1,0:T(8,128)(2,1)S(1)}) custom-call(f32[8,136,256]{2,1,0:T(8,128)S(1)} %all-to-all-done.2.got_ref, bf16[256,1088]{1,0:T(8,128)(2,1)S(1)} %get-tuple-element.312.spread_ref, bf16[128,128,256]{2,1,0:T(8,128)(2,1)} %turn_blocks.1.stored_ref, ...), custom_call_target="tpu_custom_call" | custom-call | tf_op jit(solution)/shard_map/first_products/pallas_call | solution.py:283
  28.6 16.3 %all_to_all.113.got_ref = f32[16,24,256]{2,1,0:T(8,128)S(1)} all-to-all(f32[16,24,256]{2,1,0:T(8,128)S(1)} %get-tuple-element.315), channel_id=1, replica_groups=mesh['row'=8,'col'=16] {'col'}, dimensions={0} | all-to-all | bytes 786432 | tf_op jit(solution)/shard_map/all_to_all | solution.py:26
  46.2 13.2 %all_to_all.114.got_ref = f32[8,56,256]{2,1,0:T(8,128)S(1)} all-to-all(f32[8,56,256]{2,1,0:T(8,128)S(1)} %get-tuple-element.319), channel_id=1, replica_groups=mesh['row'=8,'col'=16] {'row'}, dimensions={0} | all-to-all | bytes 917504 | tf_op jit(solution)/shard_map/all_to_all | solution.py:26
  61.3 11.6 %all_to_all.115.refs_0_ = f32[16,24,256]{2,1,0:T(8,128)S(1)} all-to-all(f32[16,24,256]{2,1,0:T(8,128)S(1)} %block_products.7), channel_id=1, replica_groups=mesh['row'=8,'col'=16] {'col'}, dimensions={0} | all-to-all | bytes 786432 | tf_op jit(solution)/shard_map/all_to_all | solution.py:26
  73.9 13.1 %all_to_all.116.got_ref = f32[8,56,256]{2,1,0:T(8,128)S(1)} all-to-all(f32[8,56,256]{2,1,0:T(8,128)S(1)} %get-tuple-element.325), channel_id=1, replica_groups=mesh['row'=8,'col'=16] {'row'}, dimensions={0} | all-to-all | bytes 917504 | tf_op jit(solution)/shard_map/all_to_all | solution.py:26
  89.0 11.6 %all_to_all.117.refs_0_ = f32[16,24,256]{2,1,0:T(8,128)S(1)} all-to-all(f32[16,24,256]{2,1,0:T(8,128)S(1)} %block_products.8), channel_id=1, replica_groups=mesh['row'=8,'col'=16] {'col'}, dimensions={0} | all-to-all | bytes 786432 | tf_op jit(solution)/shard_map/all_to_all | solution.py:26
  101.6 13.2 %all_to_all.118.got_ref = f32[8,56,256]{2,1,0:T(8,128)S(1)} all-to-all(f32[8,56,256]{2,1,0:T(8,128)S(1)} %get-tuple-element.330), channel_id=1, replica_groups=mesh['row'=8,'col'=16] {'row'}, dimensions={0} | all-to-all | bytes 917504 | tf_op jit(solution)/shard_map/all_to_all | solution.py:26
  116.7 11.6 %all_to_all.119.refs_0_ = f32[16,24,256]{2,1,0:T(8,128)S(1)} all-to-all(f32[16,24,256]{2,1,0:T(8,128)S(1)} %block_products.9), channel_id=1, replica_groups=mesh['row'=8,'col'=16] {'col'}, dimensions={0} | all-to-all | bytes 786432 | tf_op jit(solution)/shard_map/all_to_all | solution.py:26
  129.4 13.2 %all_to_all.120.got_ref = f32[8,56,256]{2,1,0:T(8,128)S(1)} all-to-all(f32[8,56,256]{2,1,0:T(8,128)S(1)} %get-tuple-element.335), channel_id=1, replica_groups=mesh['row'=8,'col'=16] {'row'}, dimensions={0} | all-to-all | bytes 917504 | tf_op jit(solution)/shard_map/all_to_all | solution.py:26
  144.5 11.6 %all_to_all.121.refs_0_ = f32[16,24,256]{2,1,0:T(8,128)S(1)} all-to-all(f32[16,24,256]{2,1,0:T(8,128)S(1)} %block_products.10), channel_id=1, replica_groups=mesh['row'=8,'col'=16] {'col'}, dimensions={0} | all-to-all | bytes 786432 | tf_op jit(solution)/shard_map/all_to_all | solution.py:26
  157.2 13.2 %all_to_all.122.got_ref = f32[8,56,256]{2,1,0:T(8,128)S(1)} all-to-all(f32[8,56,256]{2,1,0:T(8,128)S(1)} %get-tuple-element.340), channel_id=1, replica_groups=mesh['row'=8,'col'=16] {'row'}, dimensions={0} | all-to-all | bytes 917504 | tf_op jit(solution)/shard_map/all_to_all | solution.py:26
  172.3 11.6 %all_to_all.123.refs_0_ = f32[16,24,256]{2,1,0:T(8,128)S(1)} all-to-all(f32[16,24,256]{2,1,0:T(8,128)S(1)} %block_products.11), channel_id=1, replica_groups=mesh['row'=8,'col'=16] {'col'}, dimensions={0} | all-to-all | bytes 786432 | tf_op jit(solution)/shard_map/all_to_all | solution.py:26
  185.0 13.1 %all_to_all.124.got_ref = f32[8,56,256]{2,1,0:T(8,128)S(1)} all-to-all(f32[8,56,256]{2,1,0:T(8,128)S(1)} %get-tuple-element.345), channel_id=1, replica_groups=mesh['row'=8,'col'=16] {'row'}, dimensions={0} | all-to-all | bytes 917504 | tf_op jit(solution)/shard_map/all_to_all | solution.py:26
  200.1 11.6 %all_to_all.125.refs_0_ = f32[16,24,256]{2,1,0:T(8,128)S(1)} all-to-all(f32[16,24,256]{2,1,0:T(8,128)S(1)} %block_products.12), channel_id=1, replica_groups=mesh['row'=8,'col'=16] {'col'}, dimensions={0} | all-to-all | bytes 786432 | tf_op jit(solution)/shard_map/all_to_all | solution.py:26
  212.9 13.2 %all_to_all.126.got_ref = f32[8,56,256]{2,1,0:T(8,128)S(1)} all-to-all(f32[8,56,256]{2,1,0:T(8,128)S(1)} %get-tuple-element.350), channel_id=1, replica_groups=mesh['row'=8,'col'=16] {'row'}, dimensions={0} | all-to-all | bytes 917504 | tf_op jit(solution)/shard_map/all_to_all | solution.py:26
  228.0 11.6 %all_to_all.127.refs_0_ = f32[16,24,256]{2,1,0:T(8,128)S(1)} all-to-all(f32[16,24,256]{2,1,0:T(8,128)S(1)} %block_products.13), channel_id=1, replica_groups=mesh['row'=8,'col'=16] {'col'}, dimensions={0} | all-to-all | bytes 786432 | tf_op jit(solution)/shard_map/all_to_all | solution.py:26
  241.2 5.5 %all-to-all-start.18 = ((f32[128,1,256]{2,1,0:T(1,128)}), f32[128,1,256]{2,1,0:T(1,128)S(1)}, u32[]{:S(2)}, u32[]{:S(2)}) async-start(f32[128,1,256]{2,1,0:T(1,128)} %get-tuple-element.355), calls=%async_computation.18 | async-start | bytes 262144 | tf_op jit(solution)/shard_map/all_to_all | solution.py:26
  249.4 7.6 %all-to-all-done.18 = f32[128,1,256]{2,1,0:T(1,128)S(1)} async-done(((f32[128,1,256]{2,1,0:T(1,128)}), f32[128,1,256]{2,1,0:T(1,128)S(1)}, u32[]{:S(2)}, u32[]{:S(2)}) %all-to-all-start.18) | async-done | bytes 131104 | tf_op jit(solution)/shard_map/all_to_all | solution.py:26
  257.0 2.1 conditional.1
  (27 shorter events, 27.2 us)
Async XLA Ops:
  0.6 8.1 %copy-start.4 = (s32[1,256]{1,0:T(1,128)S(1)}, s32[1,256]{1,0:T(1,128)}, u32[]{:S(2)}) copy-start(s32[1,256]{1,0:T(1,128)} %cols_ref.3) | copy-start | bytes 3076
  0.6 8.1 %copy-start.5 = (s32[1,256]{1,0:T(1,128)S(1)}, s32[1,256]{1,0:T(1,128)}, u32[]{:S(2)}) copy-start(s32[1,256]{1,0:T(1,128)} %rows_ref.1) | copy-start | bytes 3076
  2.8 21.6 %all-to-all-start.2 = ((f32[8,136,256]{2,1,0:T(8,128)}), f32[8,136,256]{2,1,0:T(8,128)S(1)}, u32[]{:S(2)}, u32[]{:S(2)}) async-start(f32[8,136,256]{2,1,0:T(8,128)} %get-tuple-element.311), calls=%async_computation.2 | async-start | bytes 2228224 | tf_op jit(solution)/shard_map/all_to_all | solution.py:26
  24.4 20.5 %copy-start = (f32[16384]{0:T(1024)S(1)}, f32[16384]{0:T(1024)}, u32[]{:S(2)}) copy-start(f32[16384]{0:T(1024)} %param.16) | copy-start | bytes 196612
  239.6 17.4 %copy-start.2 = (f32[2,16384]{1,0:T(2,128)S(1)}, f32[2,16384]{1,0:T(2,128)}, u32[]{:S(2)}) copy-start(f32[2,16384]{1,0:T(2,128)} %sides_ref.1) | copy-start | bytes 393220
  241.2 15.8 %all-to-all-start.18 = ((f32[128,1,256]{2,1,0:T(1,128)}), f32[128,1,256]{2,1,0:T(1,128)S(1)}, u32[]{:S(2)}, u32[]{:S(2)}) async-start(f32[128,1,256]{2,1,0:T(1,128)} %get-tuple-element.355), calls=%async_computation.18 | async-start | bytes 262144 | tf_op jit(solution)/shard_map/all_to_all | solution.py:26

commit v4 on v3

--- a/solution.py
+++ b/solution.py
@@ -19,7 +19,7 @@
 
 epsilon = 1e-06
 
-QQ, PP, GRAM, FLAG = 9, 10, 16, 127
+QQ, PP, GRAM, FLAG, PER_SYSTEM = 9, 10, 16, 31, 32
 
 
 def swap(value, axis):
@@ -397,7 +397,7 @@
     ) - 1.0
     over = jnp.where(over | (most(present) > DST_SLOTS - 1.0), 1.0, 0.0)
     lane = lax.broadcasted_iota(jnp.int32, over_ref.shape, 1)
-    over_ref[...] = jnp.where(lane == BS + FLAG, over, 0.0)
+    over_ref[...] = jnp.where(lane == FLAG, over, 0.0)
 
 
 def open_kernel(sides_ref, cols_ref, out_ref, b_ref):
@@ -413,25 +413,32 @@
 
 
 def inner_products(dots_ref, vs, q, p, j):
-    rides = []
+    dots_ref[...] = jnp.zeros(dots_ref.shape, F32)
     for n in range(2):
         cut = slice(n * BS, (n + 1) * BS)
-        dots_ref[...] = jnp.zeros(dots_ref.shape, F32)
+        base = n * PER_SYSTEM
         qn, pn = q[:, cut], p[:, cut]
         for i in range(j):
             vn = vs[i][:, cut]
-            dots_ref[i : i + 1, :] = total(vn * pn)
-            dots_ref[GRAM + i : GRAM + i + 1, :] = total(vn * qn)
-        dots_ref[j : j + 1, :] = total(qn * pn)
-        dots_ref[QQ : QQ + 1, :] = total(qn * qn)
-        dots_ref[PP : PP + 1, :] = total(pn * pn)
-        ones = jnp.ones((8, BS), F32)
-        row = lax.dot_general(
-            ones, dots_ref[...], (((1,), (1,)), ((), ())),
-            precision=lax.Precision.HIGHEST, preferred_element_type=F32,
-        )
-        rides.append(row[0:1, :])
-    return jnp.concatenate(rides, axis=1)
+            dots_ref[base + i : base + i + 1, :] = total(vn * pn)
+            dots_ref[base + GRAM + i : base + GRAM + i + 1, :] = total(vn * qn)
+        dots_ref[base + j : base + j + 1, :] = total(qn * pn)
+        dots_ref[base + QQ : base + QQ + 1, :] = total(qn * qn)
+        dots_ref[base + PP : base + PP + 1, :] = total(pn * pn)
+    row = lax.dot_general(
+        jnp.ones((8, BS), F32), dots_ref[...], (((1,), (1,)), ((), ())),
+        precision=lax.Precision.HIGHEST, preferred_element_type=F32,
+    )[0:1, :]
+    return jnp.concatenate([row, jnp.zeros((1, BS - row.shape[1]), F32)], axis=1)
+
+
+def system_row(ride, n):
+    row = ride[:, :BS]
+    return pltpu.roll(row, BS - n * PER_SYSTEM, 1) if n else row
+
+
+def widened(row):
+    return jnp.concatenate([row, jnp.zeros_like(row)], axis=1)
 
 
 def arrived(got_ref, scatter_ref):
@@ -456,14 +463,14 @@
     b = b_ref[...]
     p = arrived(got_ref, scatter_ref) + jnp.concatenate([diag_ref[...]] * 2, axis=1) * b
     p_ref[...] = p
-    send_out(p, wanted_ref, inner_products(dots_ref, [], b, p, 0) + over_ref[0:1, :], out_ref)
+    send_out(p, wanted_ref, widened(inner_products(dots_ref, [], b, p, 0)) + over_ref[0:1, :], out_ref)
 
 
 def column_of(ride, j):
     lane = lax.broadcasted_iota(jnp.int32, (1, BS), 1)
     out = []
     for n in range(2):
-        row = ride[:, n * BS : (n + 1) * BS]
+        row = system_row(ride, n)
         inverse = 1.0 / jnp.sqrt(lane_of(row, QQ) + epsilon)
         h = row * jnp.where(lane == j, inverse * inverse, jnp.broadcast_to(inverse, (1, BS)))
         out.append((h, inverse))
@@ -498,7 +505,7 @@
     if j + 1 == STEPS - 1:
         out_ref[...] = jnp.broadcast_to(ride[:, None, :], out_ref.shape)
     else:
-        send_out(p, wanted_ref, ride, out_ref)
+        send_out(p, wanted_ref, widened(ride), out_ref)
 
 
 GRAM_AT, NUMBERS_AT = 16, 24
@@ -513,7 +520,7 @@
     known = len(rides)
     kept_ref[...] = jnp.zeros(kept_ref.shape, F32)
     for n in range(2):
-        rows = [ride[:, n * BS : (n + 1) * BS] for ride in rides]
+        rows = [system_row(ride, n) for ride in rides]
         norms = [jnp.sqrt(lane_of(row, QQ) + epsilon) for row in rows]
         inverses = [per_step[j][n][1] for j in range(known)]
         for j in range(known):
@@ -542,7 +549,7 @@
     lane = lax.broadcasted_iota(jnp.int32, (1, BS), 1)
     both = []
     for n, (h, inverse) in enumerate(column_of(ride, known)):
-        row = ride[:, n * BS : (n + 1) * BS]
+        row = system_row(ride, n)
         norm = jnp.sqrt(lane_of(row, QQ) + epsilon)
         h = jnp.where(lane <= known, h, 0.0)
         gram = jnp.where(lane < known, 2.0 * pltpu.roll(row, BS - GRAM, 1) * inverse, 0.0)
@@ -614,7 +621,7 @@
 
     out_shape = jax.ShapeDtypeStruct((rows_n, SRC_SLOTS, 2 * BS), F32)
     vec = jax.ShapeDtypeStruct((BS, 2 * BS), F32)
-    dots = pltpu.VMEM((BS, BS), F32)
+    dots = pltpu.VMEM((2 * PER_SYSTEM, BS), F32)
 
     partial, turned, wanted = first_products(got, from_whole, stored, sums, lists)
     got = swap(partial, COL)
@@ -631,7 +638,7 @@
         last = j + 1 == STEPS - 1
         outs = (
             vec, vec, vec, vec, jax.ShapeDtypeStruct((8, 2 * BS), F32),
-            jax.ShapeDtypeStruct((rows_n * cols_n, 1, 2 * BS), F32) if last else out_shape,
+            jax.ShapeDtypeStruct((rows_n * cols_n, 1, BS), F32) if last else out_shape,
         )
         v, m, q, p, ride, send = call(
             functools.partial(step_kernel, j), outs, (got, scatter, q, p, diag, wanted, *vs, *ms), [dots],
@@ -658,7 +665,7 @@
         return solution, hessenberg
 
     return lax.cond(
-        rides[0][0, BS + FLAG] > 0.0,
+        rides[0][0, FLAG] > 0.0,
         lambda *args: dense_cycle(*args[:5]),
         lambda *args: compact(*args[5:]),
         blocks, block_rows, block_cols, diagonal, right_sides, final, so_far, q, *vs,

time: 260 us -> 258 us (level)
  no operation moved by 1% of the time
where the time goes in v4:
time: 258 us
  blocking collectives  189 us (73%)
  Pallas kernels  43 us (17%)
  starting transfers between devices  11.4 us (4%)
  waiting for transfers between devices  11.1 us (4%)
    all_to_all x15, blocking collectives, swap(): return lax.all_to_all(value, axis, split_axis=0, concat_axis=0, tiled=True)  189 us
    pallas_call x19, Pallas kernels, call(): pl.pallas_call(kernel, out_shape=outs, in_specs=whole(len(operands)), out...  29.3 us
    all_to_all x2, starting transfers between devices, swap(): return lax.all_to_all(value, axis, split_axis=0, concat_axis=0, tiled=True)  11.4 us
    all_to_all x2, waiting for transfers between devices, swap(): return lax.all_to_all(value, axis, split_axis=0, concat_axis=0, tiled=True)  11.1 us
    pallas_call x1, Pallas kernels, turn_blocks(): pl.pallas_call(turn_kernel, out_shape=pltpu.MemorySpace.HBM((count // 2,...  9.53 us
  transfers between devices with their start and end apart: 2, of which 2 were waited for; matrix products, arithmetic and copies ran while one was open for 0% of the time, Pallas kernels for 5%

profile of v4, /device:TPU:1, one launch (start us, length us, event | category | flops | bytes accessed | tf_op | source)
XLA Modules:
  0.0 257.7 jit_solution(4646286630504204684)
XLA Ops:
  0.6 2.1 open.1
  2.8 6.0 %all-to-all-start.2 = ((f32[8,136,256]{2,1,0:T(8,128)}), f32[8,136,256]{2,1,0:T(8,128)S(1)}, u32[]{:S(2)}, u32[]{:S(2)}) async-start(f32[8,136,256]{2,1,0:T(8,128)} %get-tuple-element.311), calls=%async_computation.2 | async-start | bytes 2228224 | tf_op jit(solution)/shard_map/all_to_all | solution.py:26
  8.7 2.1 plan.1
  10.8 9.5 %turn_blocks.1.stored_ref = bf16[128,128,256]{2,1,0:T(8,128)(2,1)} custom-call(f32[256,128,128]{2,1,0:T(8,128)} %blocks_ref.1), custom_call_target="tpu_custom_call" | custom-call | flops 40000000 | bytes 25165824 | tf_op jit(solution)/shard_map/turn_blocks/pallas_call | solution.py:184
  20.3 4.1 %all-to-all-done.2.got_ref = f32[8,136,256]{2,1,0:T(8,128)S(1)} async-done(((f32[8,136,256]{2,1,0:T(8,128)}), f32[8,136,256]{2,1,0:T(8,128)S(1)}, u32[]{:S(2)}, u32[]{:S(2)}) %all-to-all-start.2) | async-done | bytes 1114144 | tf_op jit(solution)/shard_map/all_to_all | solution.py:26
  24.4 4.2 %first_products.1 = (f32[16,24,256]{2,1,0:T(8,128)S(1)}, bf16[128,128,256]{2,1,0:T(8,128)(2,1)S(1)}, bf16[448,128]{1,0:T(8,128)(2,1)S(1)}) custom-call(f32[8,136,256]{2,1,0:T(8,128)S(1)} %all-to-all-done.2.got_ref, bf16[256,1088]{1,0:T(8,128)(2,1)S(1)} %get-tuple-element.312.spread_ref, bf16[128,128,256]{2,1,0:T(8,128)(2,1)} %turn_blocks.1.stored_ref, ...), custom_call_target="tpu_custom_call" | custom-call | tf_op jit(solution)/shard_map/first_products/pallas_call | solution.py:283
  28.6 16.3 %all_to_all.113.got_ref = f32[16,24,256]{2,1,0:T(8,128)S(1)} all-to-all(f32[16,24,256]{2,1,0:T(8,128)S(1)} %get-tuple-element.315), channel_id=1, replica_groups=mesh['row'=8,'col'=16] {'col'}, dimensions={0} | all-to-all | bytes 786432 | tf_op jit(solution)/shard_map/all_to_all | solution.py:26
  46.0 13.2 %all_to_all.114.got_ref = f32[8,56,256]{2,1,0:T(8,128)S(1)} all-to-all(f32[8,56,256]{2,1,0:T(8,128)S(1)} %get-tuple-element.319), channel_id=1, replica_groups=mesh['row'=8,'col'=16] {'row'}, dimensions={0} | all-to-all | bytes 917504 | tf_op jit(solution)/shard_map/all_to_all | solution.py:26
  61.1 11.6 %all_to_all.115.refs_0_ = f32[16,24,256]{2,1,0:T(8,128)S(1)} all-to-all(f32[16,24,256]{2,1,0:T(8,128)S(1)} %block_products.7), channel_id=1, replica_groups=mesh['row'=8,'col'=16] {'col'}, dimensions={0} | all-to-all | bytes 786432 | tf_op jit(solution)/shard_map/all_to_all | solution.py:26
  73.6 13.1 %all_to_all.116.got_ref = f32[8,56,256]{2,1,0:T(8,128)S(1)} all-to-all(f32[8,56,256]{2,1,0:T(8,128)S(1)} %get-tuple-element.325), channel_id=1, replica_groups=mesh['row'=8,'col'=16] {'row'}, dimensions={0} | all-to-all | bytes 917504 | tf_op jit(solution)/shard_map/all_to_all | solution.py:26
  88.7 11.6 %all_to_all.117.refs_0_ = f32[16,24,256]{2,1,0:T(8,128)S(1)} all-to-all(f32[16,24,256]{2,1,0:T(8,128)S(1)} %block_products.8), channel_id=1, replica_groups=mesh['row'=8,'col'=16] {'col'}, dimensions={0} | all-to-all | bytes 786432 | tf_op jit(solution)/shard_map/all_to_all | solution.py:26
  101.2 13.2 %all_to_all.118.got_ref = f32[8,56,256]{2,1,0:T(8,128)S(1)} all-to-all(f32[8,56,256]{2,1,0:T(8,128)S(1)} %get-tuple-element.330), channel_id=1, replica_groups=mesh['row'=8,'col'=16] {'row'}, dimensions={0} | all-to-all | bytes 917504 | tf_op jit(solution)/shard_map/all_to_all | solution.py:26
  116.3 11.6 %all_to_all.119.refs_0_ = f32[16,24,256]{2,1,0:T(8,128)S(1)} all-to-all(f32[16,24,256]{2,1,0:T(8,128)S(1)} %block_products.9), channel_id=1, replica_groups=mesh['row'=8,'col'=16] {'col'}, dimensions={0} | all-to-all | bytes 786432 | tf_op jit(solution)/shard_map/all_to_all | solution.py:26
  128.8 13.2 %all_to_all.120.got_ref = f32[8,56,256]{2,1,0:T(8,128)S(1)} all-to-all(f32[8,56,256]{2,1,0:T(8,128)S(1)} %get-tuple-element.335), channel_id=1, replica_groups=mesh['row'=8,'col'=16] {'row'}, dimensions={0} | all-to-all | bytes 917504 | tf_op jit(solution)/shard_map/all_to_all | solution.py:26
  143.9 11.6 %all_to_all.121.refs_0_ = f32[16,24,256]{2,1,0:T(8,128)S(1)} all-to-all(f32[16,24,256]{2,1,0:T(8,128)S(1)} %block_products.10), channel_id=1, replica_groups=mesh['row'=8,'col'=16] {'col'}, dimensions={0} | all-to-all | bytes 786432 | tf_op jit(solution)/shard_map/all_to_all | solution.py:26
  156.5 13.1 %all_to_all.122.got_ref = f32[8,56,256]{2,1,0:T(8,128)S(1)} all-to-all(f32[8,56,256]{2,1,0:T(8,128)S(1)} %get-tuple-element.340), channel_id=1, replica_groups=mesh['row'=8,'col'=16] {'row'}, dimensions={0} | all-to-all | bytes 917504 | tf_op jit(solution)/shard_map/all_to_all | solution.py:26
  171.6 11.6 %all_to_all.123.refs_0_ = f32[16,24,256]{2,1,0:T(8,128)S(1)} all-to-all(f32[16,24,256]{2,1,0:T(8,128)S(1)} %block_products.11), channel_id=1, replica_groups=mesh['row'=8,'col'=16] {'col'}, dimensions={0} | all-to-all | bytes 786432 | tf_op jit(solution)/shard_map/all_to_all | solution.py:26
  184.2 13.1 %all_to_all.124.got_ref = f32[8,56,256]{2,1,0:T(8,128)S(1)} all-to-all(f32[8,56,256]{2,1,0:T(8,128)S(1)} %get-tuple-element.345), channel_id=1, replica_groups=mesh['row'=8,'col'=16] {'row'}, dimensions={0} | all-to-all | bytes 917504 | tf_op jit(solution)/shard_map/all_to_all | solution.py:26
  199.3 11.6 %all_to_all.125.refs_0_ = f32[16,24,256]{2,1,0:T(8,128)S(1)} all-to-all(f32[16,24,256]{2,1,0:T(8,128)S(1)} %block_products.12), channel_id=1, replica_groups=mesh['row'=8,'col'=16] {'col'}, dimensions={0} | all-to-all | bytes 786432 | tf_op jit(solution)/shard_map/all_to_all | solution.py:26
  212.0 13.2 %all_to_all.126.got_ref = f32[8,56,256]{2,1,0:T(8,128)S(1)} all-to-all(f32[8,56,256]{2,1,0:T(8,128)S(1)} %get-tuple-element.350), channel_id=1, replica_groups=mesh['row'=8,'col'=16] {'row'}, dimensions={0} | all-to-all | bytes 917504 | tf_op jit(solution)/shard_map/all_to_all | solution.py:26
  227.1 11.6 %all_to_all.127.refs_0_ = f32[16,24,256]{2,1,0:T(8,128)S(1)} all-to-all(f32[16,24,256]{2,1,0:T(8,128)S(1)} %block_products.13), channel_id=1, replica_groups=mesh['row'=8,'col'=16] {'col'}, dimensions={0} | all-to-all | bytes 786432 | tf_op jit(solution)/shard_map/all_to_all | solution.py:26
  240.2 5.4 %all-to-all-start.18 = ((f32[128,1,128]{2,1,0:T(1,128)}), f32[128,1,128]{2,1,0:T(1,128)S(1)}, u32[]{:S(2)}, u32[]{:S(2)}) async-start(f32[128,1,128]{2,1,0:T(1,128)} %get-tuple-element.355), calls=%async_computation.18 | async-start | bytes 131072 | tf_op jit(solution)/shard_map/all_to_all | solution.py:26
  248.5 7.1 %all-to-all-done.18 = f32[128,1,128]{2,1,0:T(1,128)S(1)} async-done(((f32[128,1,128]{2,1,0:T(1,128)}), f32[128,1,128]{2,1,0:T(1,128)S(1)}, u32[]{:S(2)}, u32[]{:S(2)}) %all-to-all-start.18) | async-done | bytes 65568 | tf_op jit(solution)/shard_map/all_to_all | solution.py:26
  255.5 2.1 conditional.1
  (27 shorter events, 26.4 us)
Async XLA Ops:
  0.6 8.1 %copy-start.4 = (s32[1,256]{1,0:T(1,128)S(1)}, s32[1,256]{1,0:T(1,128)}, u32[]{:S(2)}) copy-start(s32[1,256]{1,0:T(1,128)} %cols_ref.3) | copy-start | bytes 3076
  0.6 8.1 %copy-start.5 = (s32[1,256]{1,0:T(1,128)S(1)}, s32[1,256]{1,0:T(1,128)}, u32[]{:S(2)}) copy-start(s32[1,256]{1,0:T(1,128)} %rows_ref.1) | copy-start | bytes 3076
  2.8 21.6 %all-to-all-start.2 = ((f32[8,136,256]{2,1,0:T(8,128)}), f32[8,136,256]{2,1,0:T(8,128)S(1)}, u32[]{:S(2)}, u32[]{:S(2)}) async-start(f32[8,136,256]{2,1,0:T(8,128)} %get-tuple-element.311), calls=%async_computation.2 | async-start | bytes 2228224 | tf_op jit(solution)/shard_map/all_to_all | solution.py:26
  24.4 20.5 %copy-start = (f32[16384]{0:T(1024)S(1)}, f32[16384]{0:T(1024)}, u32[]{:S(2)}) copy-start(f32[16384]{0:T(1024)} %param.16) | copy-start | bytes 196612
  238.7 16.9 %copy-start.2 = (f32[2,16384]{1,0:T(2,128)S(1)}, f32[2,16384]{1,0:T(2,128)}, u32[]{:S(2)}) copy-start(f32[2,16384]{1,0:T(2,128)} %sides_ref.1) | copy-start | bytes 393220
  240.2 15.3 %all-to-all-start.18 = ((f32[128,1,128]{2,1,0:T(1,128)}), f32[128,1,128]{2,1,0:T(1,128)S(1)}, u32[]{:S(2)}, u32[]{:S(2)}) async-start(f32[128,1,128]{2,1,0:T(1,128)} %get-tuple-element.355), calls=%async_computation.18 | async-start | bytes 131072 | tf_op jit(solution)/shard_map/all_to_all | solution.py:26

commit v5 on v4

--- a/solution.py
+++ b/solution.py
@@ -220,7 +220,7 @@
         [prod_ref[pl.ds(n, count, stride=4), :] + prod_ref[pl.ds(n + 2, count, stride=4), :] for n in range(2)],
         axis=1,
     )
-    out_ref[...] = pick(sums_ref[...], products).reshape(out_ref.shape)
+    out_ref[...] = pick(sums_ref[...], products, 2).reshape(out_ref.shape)
 
 
 def first_product_kernel(
@@ -443,7 +443,7 @@
 
 def arrived(got_ref, scatter_ref):
     flat = got_ref[...].reshape(-1, 2 * BS)
-    return pick(scatter_ref[...], flat)
+    return pick(scatter_ref[...], flat, 2)
 
 
 def ridden(got_ref):

time: 258 us -> 258 us (level)
  no operation moved by 1% of the time
where the time goes in v5:
time: 258 us; the launch traced here: 257 us
  blocking collectives  190 us (74%)
  Pallas kernels  42 us (16%)
  starting transfers between devices  11.4 us (4%)
  waiting for transfers between devices  11.1 us (4%)
    all_to_all x15, blocking collectives, swap(): return lax.all_to_all(value, axis, split_axis=0, concat_axis=0, tiled=True)  190 us
    pallas_call x19, Pallas kernels, call(): pl.pallas_call(kernel, out_shape=outs, in_specs=whole(len(operands)), out...  28.3 us
    all_to_all x2, starting transfers between devices, swap(): return lax.all_to_all(value, axis, split_axis=0, concat_axis=0, tiled=True)  11.4 us
    all_to_all x2, waiting for transfers between devices, swap(): return lax.all_to_all(value, axis, split_axis=0, concat_axis=0, tiled=True)  11.1 us
    pallas_call x1, Pallas kernels, turn_blocks(): pl.pallas_call(turn_kernel, out_shape=pltpu.MemorySpace.HBM((count // 2,...  9.53 us
  transfers between devices with their start and end apart: 2, of which 2 were waited for; matrix products, arithmetic and copies ran while one was open for 0% of the time, Pallas kernels for 5%

profile of v5, /device:TPU:1, one launch (start us, length us, event | category | flops | bytes accessed | tf_op | source)
XLA Modules:
  0.0 256.9 jit_solution(15209080417936817309)
XLA Ops:
  0.6 2.1 open.1
  2.8 6.0 %all-to-all-start.2 = ((f32[8,136,256]{2,1,0:T(8,128)}), f32[8,136,256]{2,1,0:T(8,128)S(1)}, u32[]{:S(2)}, u32[]{:S(2)}) async-start(f32[8,136,256]{2,1,0:T(8,128)} %get-tuple-element.311), calls=%async_computation.2 | async-start | bytes 2228224 | tf_op jit(solution)/shard_map/all_to_all | solution.py:26
  8.7 2.1 plan.1
  10.8 9.5 %turn_blocks.1.stored_ref = bf16[128,128,256]{2,1,0:T(8,128)(2,1)} custom-call(f32[256,128,128]{2,1,0:T(8,128)} %blocks_ref.1), custom_call_target="tpu_custom_call" | custom-call | flops 40000000 | bytes 25165824 | tf_op jit(solution)/shard_map/turn_blocks/pallas_call | solution.py:184
  20.3 4.1 %all-to-all-done.2.got_ref = f32[8,136,256]{2,1,0:T(8,128)S(1)} async-done(((f32[8,136,256]{2,1,0:T(8,128)}), f32[8,136,256]{2,1,0:T(8,128)S(1)}, u32[]{:S(2)}, u32[]{:S(2)}) %all-to-all-start.2) | async-done | bytes 1114144 | tf_op jit(solution)/shard_map/all_to_all | solution.py:26
  24.4 4.1 %first_products.1 = (f32[16,24,256]{2,1,0:T(8,128)S(1)}, bf16[128,128,256]{2,1,0:T(8,128)(2,1)S(1)}, bf16[448,128]{1,0:T(8,128)(2,1)S(1)}) custom-call(f32[8,136,256]{2,1,0:T(8,128)S(1)} %all-to-all-done.2.got_ref, bf16[256,1088]{1,0:T(8,128)(2,1)S(1)} %get-tuple-element.312.spread_ref, bf16[128,128,256]{2,1,0:T(8,128)(2,1)} %turn_blocks.1.stored_ref, ...), custom_call_target="tpu_custom_call" | custom-call | tf_op jit(solution)/shard_map/first_products/pallas_call | solution.py:283
  28.5 16.3 %all_to_all.113.got_ref = f32[16,24,256]{2,1,0:T(8,128)S(1)} all-to-all(f32[16,24,256]{2,1,0:T(8,128)S(1)} %get-tuple-element.315), channel_id=1, replica_groups=mesh['row'=8,'col'=16] {'col'}, dimensions={0} | all-to-all | bytes 786432 | tf_op jit(solution)/shard_map/all_to_all | solution.py:26
  45.8 13.2 %all_to_all.114.got_ref = f32[8,56,256]{2,1,0:T(8,128)S(1)} all-to-all(f32[8,56,256]{2,1,0:T(8,128)S(1)} %get-tuple-element.319), channel_id=1, replica_groups=mesh['row'=8,'col'=16] {'row'}, dimensions={0} | all-to-all | bytes 917504 | tf_op jit(solution)/shard_map/all_to_all | solution.py:26
  60.9 11.6 %all_to_all.115.refs_0_ = f32[16,24,256]{2,1,0:T(8,128)S(1)} all-to-all(f32[16,24,256]{2,1,0:T(8,128)S(1)} %block_products.7), channel_id=1, replica_groups=mesh['row'=8,'col'=16] {'col'}, dimensions={0} | all-to-all | bytes 786432 | tf_op jit(solution)/shard_map/all_to_all | solution.py:26
  73.2 13.1 %all_to_all.116.got_ref = f32[8,56,256]{2,1,0:T(8,128)S(1)} all-to-all(f32[8,56,256]{2,1,0:T(8,128)S(1)} %get-tuple-element.325), channel_id=1, replica_groups=mesh['row'=8,'col'=16] {'row'}, dimensions={0} | all-to-all | bytes 917504 | tf_op jit(solution)/shard_map/all_to_all | solution.py:26
  88.3 11.6 %all_to_all.117.refs_0_ = f32[16,24,256]{2,1,0:T(8,128)S(1)} all-to-all(f32[16,24,256]{2,1,0:T(8,128)S(1)} %block_products.8), channel_id=1, replica_groups=mesh['row'=8,'col'=16] {'col'}, dimensions={0} | all-to-all | bytes 786432 | tf_op jit(solution)/shard_map/all_to_all | solution.py:26
  100.7 13.1 %all_to_all.118.got_ref = f32[8,56,256]{2,1,0:T(8,128)S(1)} all-to-all(f32[8,56,256]{2,1,0:T(8,128)S(1)} %get-tuple-element.330), channel_id=1, replica_groups=mesh['row'=8,'col'=16] {'row'}, dimensions={0} | all-to-all | bytes 917504 | tf_op jit(solution)/shard_map/all_to_all | solution.py:26
  115.8 11.6 %all_to_all.119.refs_0_ = f32[16,24,256]{2,1,0:T(8,128)S(1)} all-to-all(f32[16,24,256]{2,1,0:T(8,128)S(1)} %block_products.9), channel_id=1, replica_groups=mesh['row'=8,'col'=16] {'col'}, dimensions={0} | all-to-all | bytes 786432 | tf_op jit(solution)/shard_map/all_to_all | solution.py:26
  128.2 13.2 %all_to_all.120.got_ref = f32[8,56,256]{2,1,0:T(8,128)S(1)} all-to-all(f32[8,56,256]{2,1,0:T(8,128)S(1)} %get-tuple-element.335), channel_id=1, replica_groups=mesh['row'=8,'col'=16] {'row'}, dimensions={0} | all-to-all | bytes 917504 | tf_op jit(solution)/shard_map/all_to_all | solution.py:26
  143.3 11.6 %all_to_all.121.refs_0_ = f32[16,24,256]{2,1,0:T(8,128)S(1)} all-to-all(f32[16,24,256]{2,1,0:T(8,128)S(1)} %block_products.10), channel_id=1, replica_groups=mesh['row'=8,'col'=16] {'col'}, dimensions={0} | all-to-all | bytes 786432 | tf_op jit(solution)/shard_map/all_to_all | solution.py:26
  155.8 13.3 %all_to_all.122.got_ref = f32[8,56,256]{2,1,0:T(8,128)S(1)} all-to-all(f32[8,56,256]{2,1,0:T(8,128)S(1)} %get-tuple-element.340), channel_id=1, replica_groups=mesh['row'=8,'col'=16] {'row'}, dimensions={0} | all-to-all | bytes 917504 | tf_op jit(solution)/shard_map/all_to_all | solution.py:26
  171.0 11.6 %all_to_all.123.refs_0_ = f32[16,24,256]{2,1,0:T(8,128)S(1)} all-to-all(f32[16,24,256]{2,1,0:T(8,128)S(1)} %block_products.11), channel_id=1, replica_groups=mesh['row'=8,'col'=16] {'col'}, dimensions={0} | all-to-all | bytes 786432 | tf_op jit(solution)/shard_map/all_to_all | solution.py:26
  183.6 13.2 %all_to_all.124.got_ref = f32[8,56,256]{2,1,0:T(8,128)S(1)} all-to-all(f32[8,56,256]{2,1,0:T(8,128)S(1)} %get-tuple-element.345), channel_id=1, replica_groups=mesh['row'=8,'col'=16] {'row'}, dimensions={0} | all-to-all | bytes 917504 | tf_op jit(solution)/shard_map/all_to_all | solution.py:26
  198.6 11.6 %all_to_all.125.refs_0_ = f32[16,24,256]{2,1,0:T(8,128)S(1)} all-to-all(f32[16,24,256]{2,1,0:T(8,128)S(1)} %block_products.12), channel_id=1, replica_groups=mesh['row'=8,'col'=16] {'col'}, dimensions={0} | all-to-all | bytes 786432 | tf_op jit(solution)/shard_map/all_to_all | solution.py:26
  211.2 13.2 %all_to_all.126.got_ref = f32[8,56,256]{2,1,0:T(8,128)S(1)} all-to-all(f32[8,56,256]{2,1,0:T(8,128)S(1)} %get-tuple-element.350), channel_id=1, replica_groups=mesh['row'=8,'col'=16] {'row'}, dimensions={0} | all-to-all | bytes 917504 | tf_op jit(solution)/shard_map/all_to_all | solution.py:26
  226.2 11.6 %all_to_all.127.refs_0_ = f32[16,24,256]{2,1,0:T(8,128)S(1)} all-to-all(f32[16,24,256]{2,1,0:T(8,128)S(1)} %block_products.13), channel_id=1, replica_groups=mesh['row'=8,'col'=16] {'col'}, dimensions={0} | all-to-all | bytes 786432 | tf_op jit(solution)/shard_map/all_to_all | solution.py:26
  239.4 5.4 %all-to-all-start.18 = ((f32[128,1,128]{2,1,0:T(1,128)}), f32[128,1,128]{2,1,0:T(1,128)S(1)}, u32[]{:S(2)}, u32[]{:S(2)}) async-start(f32[128,1,128]{2,1,0:T(1,128)} %get-tuple-element.355), calls=%async_computation.18 | async-start | bytes 131072 | tf_op jit(solution)/shard_map/all_to_all | solution.py:26
  247.6 7.1 %all-to-all-done.18 = f32[128,1,128]{2,1,0:T(1,128)S(1)} async-done(((f32[128,1,128]{2,1,0:T(1,128)}), f32[128,1,128]{2,1,0:T(1,128)S(1)}, u32[]{:S(2)}, u32[]{:S(2)}) %all-to-all-start.18) | async-done | bytes 65568 | tf_op jit(solution)/shard_map/all_to_all | solution.py:26
  254.7 2.1 conditional.1
  (27 shorter events, 25.4 us)
Async XLA Ops:
  0.6 8.1 %copy-start.4 = (s32[1,256]{1,0:T(1,128)S(1)}, s32[1,256]{1,0:T(1,128)}, u32[]{:S(2)}) copy-start(s32[1,256]{1,0:T(1,128)} %cols_ref.3) | copy-start | bytes 3076
  0.6 8.1 %copy-start.5 = (s32[1,256]{1,0:T(1,128)S(1)}, s32[1,256]{1,0:T(1,128)}, u32[]{:S(2)}) copy-start(s32[1,256]{1,0:T(1,128)} %rows_ref.1) | copy-start | bytes 3076
  2.8 21.6 %all-to-all-start.2 = ((f32[8,136,256]{2,1,0:T(8,128)}), f32[8,136,256]{2,1,0:T(8,128)S(1)}, u32[]{:S(2)}, u32[]{:S(2)}) async-start(f32[8,136,256]{2,1,0:T(8,128)} %get-tuple-element.311), calls=%async_computation.2 | async-start | bytes 2228224 | tf_op jit(solution)/shard_map/all_to_all | solution.py:26
  24.4 20.5 %copy-start = (f32[16384]{0:T(1024)S(1)}, f32[16384]{0:T(1024)}, u32[]{:S(2)}) copy-start(f32[16384]{0:T(1024)} %param.16) | copy-start | bytes 196612
  237.8 16.9 %copy-start.2 = (f32[2,16384]{1,0:T(2,128)S(1)}, f32[2,16384]{1,0:T(2,128)}, u32[]{:S(2)}) copy-start(f32[2,16384]{1,0:T(2,128)} %sides_ref.1) | copy-start | bytes 393220
  239.4 15.4 %all-to-all-start.18 = ((f32[128,1,128]{2,1,0:T(1,128)}), f32[128,1,128]{2,1,0:T(1,128)S(1)}, u32[]{:S(2)}, u32[]{:S(2)}) async-start(f32[128,1,128]{2,1,0:T(1,128)} %get-tuple-element.355), calls=%async_computation.18 | async-start | bytes 131072 | tf_op jit(solution)/shard_map/all_to_all | solution.py:26
